TPU v7x, 128 devices: a whole 4x4x4 slice. The times are simulated.
128 devices in a mesh: vocab: 32 (over x, z, core), group: 4 (over y).
Axes of the slice: x: 4, y: 4, z: 4, core: 2. Of those that a mesh axis runs over, the one named last changes fastest.
Arguments:
- hidden_states: bfloat16 [2048, 4096], P(('group', 'vocab')), parts along dimension 0, may hold values from -32 to 32
- head_weight: bfloat16 [4096, 77824], P(None, 'vocab'), may hold values from -1 to 1
- pick_index: int32 [2048, 64], P('group'), parts along dimension 0, may hold values from 0 to 77823, as said below
- owner_order: int32 [2048], P('group'), parts along dimension 0, may hold values from 0 to 511, each once
Outputs:
- token_logprobs: float32 [2048, 64], P(('group', 'vocab')), parts along dimension 0
- token_logtotal: float32 [2048], P(('group', 'vocab')), parts along dimension 0
There are 4 independent parts, one for each index of `group`. A program takes and returns all parts, laid end to end along the dimension named above; an argument that names none is the same for every part. Nothing has to cross between parts.
Inputs may be any that keep to these rules, and one draw needn't show every extreme that they name: `pick_index`: each row holds 64 distinct vocabulary entries. `owner_order`: each token appears once.
All inputs are finite; a program needn't handle non-finite values.
Results may differ from a plain program's by a relative error of at most 0.0003.
Values may be sent and summed in bfloat16 or wider, within the bound.
No kernel may reach another device: no remote copies, remote signals or barrier semaphores. Data moves between devices by JAX's collectives and lax.ppermute only.
A program may use at most 128 MiB of HBM per device.

v0:
```python
import functools

import jax
import jax.numpy as jnp
import numpy as np
from jax import lax
from jax.experimental import pallas as pl
from jax.experimental.pallas import tpu as pltpu
from jax.sharding import PartitionSpec as P


LANES = 128
ROWS = 8
RING = 4
CORES = 2
TILE = 512
AXIS = "vocab"
STEPS = (0, 1, 3, 2)
AHEAD = 3
SETTLE_FLOPS = 1 << 34


def index_of(x, z, core):
    return (x * RING + z) * CORES + core


def place_of(index):
    return index >> 3, (index >> 1) & 3, index & 1


def pairs(target):
    return [
        (index_of(x, z, c), index_of(*target(x, z, c)))
        for x in range(RING)
        for z in range(RING)
        for c in range(CORES)
    ]


def along(step, first_axis_core):
    return pairs(
        lambda x, z, c: ((x + step) % RING, z, c)
        if c == first_axis_core
        else (x, (z + step) % RING, c)
    )


def settle(blocks):
    def kernel(blocks_ref, out_ref):
        out_ref[...] = blocks_ref[...]

    vector = pl.BlockSpec(memory_space=pltpu.VMEM)
    return pl.pallas_call(
        kernel,
        out_shape=jax.ShapeDtypeStruct(blocks.shape, blocks.dtype),
        in_specs=[vector],
        out_specs=vector,
        compiler_params=pltpu.CompilerParams(vmem_limit_bytes=1024 * 1024),
        cost_estimate=pl.CostEstimate(
            flops=SETTLE_FLOPS, bytes_accessed=1024, transcendentals=0
        ),
    )(blocks)


def gathered_blocks(mine, arrivals):
    x, z, c = place_of(mine)
    at = np.array([(STEPS[second], STEPS[first], other) for second, first, other in arrivals])
    second, first, other = (jnp.asarray(v, jnp.int32) for v in at.T)
    core = c ^ other
    from_x = (x - jnp.where(core == 0, first, second)) & 3
    from_z = (z - jnp.where(core == 0, second, first)) & 3
    return index_of(from_x, from_z, core)


def chunk_kernel(*refs, pieces, blocks, ahead, loads, last):
    refs = list(refs)

    def take(n):
        taken, refs[:n] = refs[:n], []
        return taken

    (block_ref,) = take(1)
    if last:
        (order_ref,) = take(1)
    x_refs, held_refs = take(pieces), take(ahead)
    weight_ref, index_ref, out_ref = take(3)
    if loads:
        source_ref, picks_ref = weight_ref, index_ref
        weight_ref, index_ref = take(2)
    x_all, index_here, even, odd, top_ref, sum_ref, found_ref = take(7)
    count = x_all.shape[0]
    width = weight_ref.shape[1]
    edges = [(left, min(left + TILE, width)) for left in range(0, width, TILE)]
    copies = []
    if loads:
        (done,) = take(1)
        copies = [
            pltpu.make_async_copy(source_ref.at[:, l:r], weight_ref.at[:, l:r], done.at[t])
            for t, (l, r) in enumerate(edges)
        ]
        for copy in copies[:AHEAD]:
            copy.start()
    if loads:
        picks, tokens = picks_ref.shape
        for left in range(0, tokens, LANES):
            some = picks_ref[:, left : left + LANES]
            more = jnp.full((LANES - picks, LANES), -1, jnp.int32)
            index_ref[left : left + LANES, :] = jnp.concatenate([some, more], axis=0).T
    at = 0
    for x_ref in x_refs:
        x_all[at : at + x_ref.shape[0], :] = x_ref[...]
        at += x_ref.shape[0]
    block_rows = index_ref.shape[0] // block_ref.shape[0]

    def rows_of(block):
        return pl.ds(pl.multiple_of(block_ref[block] * block_rows, block_rows), block_rows)

    start = lax.axis_index(AXIS) * width
    for b, block in enumerate(blocks):
        index_here[b * block_rows : (b + 1) * block_rows, :] = index_ref[rows_of(block), :] - start

    def fold(logits, tile, columns):
        for b in range(count // ROWS):
            rows = slice(b * ROWS, (b + 1) * ROWS)
            wanted = index_here[rows, :]
            wanted_tile = lax.shift_right_arithmetic(wanted, 7)
            wanted_lane = lax.bitwise_and(wanted, LANES - 1)
            parts = [logits[rows, j * LANES : (j + 1) * LANES] for j in range(columns)]
            top = functools.reduce(jnp.maximum, parts)
            if tile:
                before = top_ref[rows, :]
                top = jnp.maximum(before, top)
            total = functools.reduce(jnp.add, [jnp.exp(p - top) for p in parts])
            if tile:
                total = total + sum_ref[rows, :] * jnp.exp(before - top)
                found = found_ref[rows, :]
            else:
                found = jnp.zeros((ROWS, LANES), jnp.float32)
            for j, part in enumerate(parts):
                seen = jnp.take_along_axis(part, wanted_lane, axis=1, mode="promise_in_bounds")
                found = jnp.where(wanted_tile == tile + j, seen, found)
            top_ref[rows, :] = top
            sum_ref[rows, :] = total
            found_ref[rows, :] = found

    waiting = None
    for t, (left, right) in enumerate(edges):
        if copies:
            copies[t].wait()
            if t + AHEAD < len(copies):
                copies[t + AHEAD].start()
        logits = (even, odd)[t % 2]
        logits[:, : right - left] = jnp.dot(
            x_all[...], weight_ref[:, left:right], preferred_element_type=jnp.float32
        )
        if waiting is not None:
            fold(*waiting)
        waiting = (logits, left // LANES, (right - left) // LANES)
    fold(*waiting)
    lane = lax.broadcasted_iota(jnp.int32, (ROWS, LANES), 1)
    rest = out_ref
    if last:
        held, rest = take(2)
    for b in range(count // ROWS):
        rows = slice(b * ROWS, (b + 1) * ROWS)
        tops = top_ref[rows, :]
        top = jnp.max(tops, axis=1, keepdims=True)
        total = jnp.sum(sum_ref[rows, :] * jnp.exp(tops - top), axis=1, keepdims=True)
        found = jnp.where(lane == LANES - 2, top, found_ref[rows, :])
        rest[rows, :] = jnp.where(lane == LANES - 1, total, found)
    if last:
        block = 0
        for held_ref in [*held_refs, rest]:
            for at in range(0, held_ref.shape[0], block_rows):
                held[rows_of(block), :] = held_ref[at : at + block_rows, :]
                block += 1
    if last:
        unroll = 16

        def move(b, _):
            for i in range(unroll):
                r = b * unroll + i
                out_ref[pl.ds(r, 1), :] = held[pl.ds(order_ref[r], 1), :]
            return 0

        lax.fori_loop(0, out_ref.shape[0] // unroll, move, 0)


def chunk(blocks, xs, members, held, weight, index, order=None, loads=False):
    last = order is not None
    count = sum(x.shape[0] for x in xs)
    depth, width = weight.shape
    tokens = index.shape[1 if loads else 0]
    scalar = pl.BlockSpec(memory_space=pltpu.SMEM)
    vector = pl.BlockSpec(memory_space=pltpu.VMEM)
    rows = pltpu.VMEM((count, LANES), jnp.float32)
    out_shape = [jax.ShapeDtypeStruct((tokens if last else count, LANES), jnp.float32)]
    scratch = [
        pltpu.VMEM((count, depth), jnp.bfloat16),
        pltpu.VMEM((count, LANES), jnp.int32),
        pltpu.VMEM((count, TILE), jnp.float32),
        pltpu.VMEM((count, TILE), jnp.float32),
        rows,
        rows,
        rows,
    ]
    if loads:
        out_shape.append(jax.ShapeDtypeStruct((depth, width), weight.dtype))
        out_shape.append(jax.ShapeDtypeStruct((tokens, LANES), jnp.int32))
        scratch.append(pltpu.SemaphoreType.DMA((pl.cdiv(width, TILE),)))
    if last:
        scratch += [pltpu.VMEM((tokens, LANES), jnp.float32), rows]
    out = pl.pallas_call(
        functools.partial(
            chunk_kernel,
            pieces=len(xs),
            blocks=members,
            ahead=len(held),
            loads=loads,
            last=last,
        ),
        out_shape=out_shape,
        in_specs=[scalar] * (2 if last else 1)
        + [vector] * (len(xs) + len(held))
        + [pl.BlockSpec(memory_space=pltpu.HBM) if loads else vector, vector],
        out_specs=[vector] * len(out_shape),
        scratch_shapes=scratch,
        compiler_params=pltpu.CompilerParams(
            vmem_limit_bytes=(22 if loads else 16) * 1024 * 1024
        ),
        cost_estimate=pl.CostEstimate(
            flops=2 * count * depth * width,
            bytes_accessed=2 * depth * width,
            transcendentals=count * width,
        ),
    )(blocks, *([order] if last else []), *xs, *held, weight, index)
    return out if loads else out[0]


def combine_kernel(rows_ref, logprobs_ref, log_total_ref):
    rows = rows_ref[...]
    shards, own, _ = rows.shape
    shifted = pltpu.roll(rows.reshape(shards * own, LANES), 1, 1).reshape(rows.shape)
    top = jnp.max(shifted, axis=0)
    total = jnp.sum(rows * jnp.exp(shifted - top[None]), axis=0)
    lane = lax.broadcasted_iota(jnp.int32, (own, LANES), 1)
    log_total = jnp.where(lane == LANES - 1, top + jnp.log(total), 0.0)
    log_total = jnp.sum(log_total, axis=1, keepdims=True)
    picks = logprobs_ref.shape[1]
    logprobs_ref[...] = jnp.sum(rows, axis=0)[:, :picks] - log_total
    row = lax.broadcasted_iota(jnp.int32, (own, LANES), 0)
    line = jnp.sum(jnp.where(row == lane, log_total, 0.0), axis=0, keepdims=True)
    log_total_ref[...] = line[:, :own]


def combine(rows, picks):
    own = rows.shape[1]
    vector = pl.BlockSpec(memory_space=pltpu.VMEM)
    logprobs, log_total = pl.pallas_call(
        combine_kernel,
        out_shape=[
            jax.ShapeDtypeStruct((own, picks), jnp.float32),
            jax.ShapeDtypeStruct((1, own), jnp.float32),
        ],
        in_specs=[vector],
        out_specs=[vector, vector],
        compiler_params=pltpu.CompilerParams(vmem_limit_bytes=4 * 1024 * 1024),
    )(rows)
    return logprobs, log_total.reshape(own)


def shifts(value, phase):
    received = []
    for k in STEPS[1:]:
        received.append(lax.ppermute(value, AXIS, along(k, phase)))
    return received


def program(hidden_states, head_weight, pick_index, owner_order):
    shard_count = lax.axis_size(AXIS)
    mine = lax.axis_index(AXIS)
    own_rows = hidden_states.shape[0]
    pick_count = pick_index.shape[1]
    swap = pairs(lambda x, z, c: (x, z, 1 - c))

    def swapped(value):
        return lax.ppermute(value, AXIS, swap)

    own = hidden_states
    line = jnp.concatenate(shifts(own, 0))
    cross = jnp.concatenate(shifts(own, 1))
    rest = shifts(line, 1)
    early = {"own": own, "line": line, "cross": cross}
    steps = range(1, RING)
    members = [(0, 0)] + [(0, i) for i in steps] + [(j, 0) for j in steps]
    late = [(j, i) for j in steps for i in steps]
    arrivals = [
        (j, i, other) for group in (members, late) for other in (0, 1) for j, i in group
    ]
    blocks = settle(gathered_blocks(mine, arrivals))
    at = list(range(shard_count))
    cut = 2 * len(members), 2 * len(members) + len(late)
    others = [swapped(v) for v in early.values()]
    xs = [*early.values(), *others]
    first, weight, index = chunk(
        blocks, xs, at[: cut[0]], [], head_weight, pick_index.T, loads=True
    )
    *rest, first = lax.optimization_barrier((*rest, first))
    second = chunk(blocks, rest, at[cut[0] : cut[1]], [], weight, index)
    others = [swapped(v) for v in rest]
    held = [first, second]
    rows = chunk(blocks, others, at[cut[1] :], held, weight, index, order=owner_order)
    rows = rows.reshape(shard_count, own_rows, LANES)
    received = lax.all_to_all(rows, AXIS, split_axis=0, concat_axis=0, tiled=True)
    return combine(received, pick_count)


def solution(mesh):
    in_specs = (P(("group", "vocab"), None), P(None, "vocab"), P("group", None), P("group"))
    out_specs = (P(("group", "vocab"), None), P(("group", "vocab")))
    return jax.shard_map(
        program, mesh=mesh, in_specs=in_specs, out_specs=out_specs, check_vma=False
    )
```

profile of v0, /device:TPU:1, one launch (start us, length us, event | category | flops | bytes accessed | tf_op | source)
XLA Modules:
  0.0 58.0 jit_solution(17826471719700984698)
XLA Ops:
  0.6 2.5 %collective-permute-start = (bf16[16,4096]{1,0:T(8,128)(2,1)}, bf16[16,4096]{1,0:T(8,128)(2,1)S(1)}, u32[]{:S(2)}, u32[]{:S(2)}) collective-permute-start(bf16[16,4096]{1,0:T(8,128)(2,1)} %refs_1_.2), channel_id=1, source_target_pairs={{0,32},{4,12},{8,40},{12,20},{16,48},{20,28},{24,56},{28,4},{32,64... | collective-permute-start | bytes 393224 | tf_op jit(solution)/shard_map/ppermute | solution.py:275
  3.2 2.2 %collective-permute-start.1 = (bf16[16,4096]{1,0:T(8,128)(2,1)}, bf16[16,4096]{1,0:T(8,128)(2,1)S(1)}, u32[]{:S(2)}, u32[]{:S(2)}) collective-permute-start(bf16[16,4096]{1,0:T(8,128)(2,1)} %refs_1_.2), channel_id=1, source_target_pairs={{0,96},{4,28},{8,104},{12,4},{16,112},{20,12},{24,120},{28,20},{32... | collective-permute-start | bytes 393224 | tf_op jit(solution)/shard_map/ppermute | solution.py:275
  5.4 1.2 %collective-permute-start.2 = (bf16[16,4096]{1,0:T(8,128)(2,1)}, bf16[16,4096]{1,0:T(8,128)(2,1)S(1)}, u32[]{:S(2)}, u32[]{:S(2)}) collective-permute-start(bf16[16,4096]{1,0:T(8,128)(2,1)} %refs_1_.2), channel_id=1, source_target_pairs={{0,64},{4,20},{8,72},{12,28},{16,80},{20,4},{24,88},{28,12},{32,96... | collective-permute-start | bytes 393224 | tf_op jit(solution)/shard_map/ppermute | solution.py:275
  6.6 1.2 %collective-permute-start.6 = (bf16[16,4096]{1,0:T(8,128)(2,1)}, bf16[16,4096]{1,0:T(8,128)(2,1)S(1)}, u32[]{:S(2)}, u32[]{:S(2)}) collective-permute-start(bf16[16,4096]{1,0:T(8,128)(2,1)} %refs_1_.2), channel_id=1, source_target_pairs={{0,8},{4,36},{8,16},{12,44},{16,24},{20,52},{24,0},{28,60},{32,40}... | collective-permute-start | bytes 393224 | tf_op jit(solution)/shard_map/ppermute | solution.py:275
  7.8 1.5 %collective-permute-start.7 = (bf16[16,4096]{1,0:T(8,128)(2,1)}, bf16[16,4096]{1,0:T(8,128)(2,1)S(1)}, u32[]{:S(2)}, u32[]{:S(2)}) collective-permute-start(bf16[16,4096]{1,0:T(8,128)(2,1)} %refs_1_.2), channel_id=1, source_target_pairs={{0,24},{4,100},{8,0},{12,108},{16,8},{20,116},{24,16},{28,124},{32... | collective-permute-start | bytes 393224 | tf_op jit(solution)/shard_map/ppermute | solution.py:275
  9.3 0.7 %xor_add_fusion.blocks_ref = s32[32]{0:T(128)S(1)} fusion(s32[32]{0:T(128)} %constant.25.clone, s32[32]{0:T(128)} %constant.23.clone, s32[32]{0:T(128)} %constant.24.clone, s32[]{:T(128)S(6)} %and.15, s32[]{:T(128)S(6)} %and.13, s32[]{:T(128)S(6)} %shift_right_arithmetic.6), kind=kLoop, calls=%fused_computation.8 | loop fusion | flops 384 | bytes 524 | tf_op jit(solution)/shard_map/add | solution.py:24
  10.0 0.0 collective-permute-done
  10.0 1.6 %collective-permute-start.8 = (bf16[16,4096]{1,0:T(8,128)(2,1)}, bf16[16,4096]{1,0:T(8,128)(2,1)S(1)}, u32[]{:S(2)}, u32[]{:S(2)}) collective-permute-start(bf16[16,4096]{1,0:T(8,128)(2,1)} %refs_1_.2), channel_id=1, source_target_pairs={{0,16},{4,68},{8,24},{12,76},{16,0},{20,84},{24,8},{28,92},{32,48}... | collective-permute-start | bytes 393224 | tf_op jit(solution)/shard_map/ppermute | solution.py:275
  11.6 0.0 collective-permute-done.1
  11.6 2.4 %collective-permute-start.9 = (bf16[16,4096]{1,0:T(8,128)(2,1)}, bf16[16,4096]{1,0:T(8,128)(2,1)S(1)}, u32[]{:S(2)}, u32[]{:S(2)}) collective-permute-start(bf16[16,4096]{1,0:T(8,128)(2,1)} %refs_1_.2), channel_id=1, source_target_pairs={{0,4},{4,0},{8,12},{12,8},{16,20},{20,16},{24,28},{28,24},{32,36},... | collective-permute-start | bytes 393224 | tf_op jit(solution)/shard_map/ppermute | solution.py:287
  14.0 0.0 collective-permute-done.2
  14.1 0.1 collective-permute-start.10
  14.2 0.0 collective-permute-done.6
  14.2 0.0 collective-permute-done.7
  14.2 1.3 %collective-permute-done.8 = bf16[16,4096]{1,0:T(8,128)(2,1)S(1)} collective-permute-done((bf16[16,4096]{1,0:T(8,128)(2,1)}, bf16[16,4096]{1,0:T(8,128)(2,1)S(1)}, u32[]{:S(2)}, u32[]{:S(2)}) %collective-permute-start.8) | collective-permute-done | bytes 131104 | tf_op jit(solution)/shard_map/ppermute | solution.py:275
  15.6 0.0 copy-start
  15.6 0.0 copy-start.1
  15.6 3.3 %collective-permute-start.11 = (bf16[48,4096]{1,0:T(8,128)(2,1)S(1)}, bf16[48,4096]{1,0:T(8,128)(2,1)S(1)}, u32[]{:S(2)}, u32[]{:S(2)}) collective-permute-start(bf16[48,4096]{1,0:T(8,128)(2,1)S(1)} %constant_dynamic-update-slice_fusion.3.refs_3_), channel_id=1, source_target_pairs={{0,4},{4,0},{8,12},{12,8},{16,20},{20,16},{24,28},{28,24},{32,36},... | collective-permute-start | bytes 1179656 | tf_op jit(solution)/shard_map/ppermute | solution.py:287
  18.9 0.3 collective-permute-start.3
  19.2 2.4 %collective-permute-start.4 = (bf16[48,4096]{1,0:T(8,128)(2,1)S(1)}, bf16[48,4096]{1,0:T(8,128)(2,1)S(1)}, u32[]{:S(2)}, u32[]{:S(2)}) collective-permute-start(bf16[48,4096]{1,0:T(8,128)(2,1)S(1)} %constant_dynamic-update-slice_fusion.refs_2_), channel_id=1, source_target_pairs={{0,24},{4,100},{8,0},{12,108},{16,8},{20,116},{24,16},{28,124},{32... | collective-permute-start | bytes 1179656 | tf_op jit(solution)/shard_map/ppermute | solution.py:275
  21.5 0.0 collective-permute-done.9.refs_4_
  21.5 0.2 collective-permute-start.5
  21.8 0.0 collective-permute-done.10.refs_5_
  21.8 0.0 collective-permute-done.11.refs_6_
  21.8 0.0 copy-done
  21.8 0.0 copy-done.1
  21.8 0.0 copy-start.2
  21.8 9.7 %shard_map.87 = (f32[224,128]{1,0:T(8,128)S(1)}, bf16[4096,2432]{1,0:T(8,128)(2,1)S(1)}, s32[512,128]{1,0:T(8,128)S(1)}) custom-call(s32[32]{0:T(128)S(1)} %shard_map.86.refs_0_, bf16[16,4096]{1,0:T(8,128)(2,1)S(1)} %copy-done, bf16[48,4096]{1,0:T(8,128)(2,1)S(1)} %constant_dynamic-update-slice_fusion.refs_2_, ...), custom_call_target="tpu_custom_call" | custom-call | flops 4462739456 | bytes 19922944 | tf_op jit(solution)/shard_map/pallas_call | solution.py:213
  31.5 0.0 collective-permute-done.3.refs_1_
  31.5 0.0 collective-permute-done.4.refs_2_
  31.5 0.0 collective-permute-done.5.refs_3_
  31.5 1.2 %collective-permute-start.12 = (bf16[48,4096]{1,0:T(8,128)(2,1)S(1)}, bf16[48,4096]{1,0:T(8,128)(2,1)S(1)}, u32[]{:S(2)}, u32[]{:S(2)}) collective-permute-start(bf16[48,4096]{1,0:T(8,128)(2,1)S(1)} %collective-permute-done.3.refs_1_), channel_id=1, source_target_pairs={{0,4},{4,0},{8,12},{12,8},{16,20},{20,16},{24,28},{28,24},{32,36},... | collective-permute-start | bytes 1179656 | tf_op jit(solution)/shard_map/ppermute | solution.py:287
  32.7 0.1 collective-permute-start.13
  32.8 0.4 collective-permute-start.14
  33.2 4.5 %shard_map.88.refs_6_ = f32[144,128]{1,0:T(8,128)S(1)} custom-call(s32[32]{0:T(128)S(1)} %shard_map.86.refs_0_, bf16[48,4096]{1,0:T(8,128)(2,1)S(1)} %collective-permute-done.3.refs_1_, bf16[48,4096]{1,0:T(8,128)(2,1)S(1)} %collective-permute-done.4.refs_2_, bf16[48,4096]{1,0:T(8,128)(2,1)S(1)} %collective-permute-done.5.refs_3_, ...), custom_call_target="tpu_custom_call" | custom-call | flops 2868903936 | bytes 19922944 | tf_op jit(solution)/shard_map/pallas_call | solution.py:213
  37.7 0.0 collective-permute-done.12.refs_2_
  37.7 0.0 collective-permute-done.13.refs_3_
  37.7 0.0 collective-permute-done.14.refs_4_
  37.7 0.0 copy-done.2
  37.7 5.0 %shard_map.89 = f32[512,128]{1,0:T(8,128)S(1)} custom-call(s32[32]{0:T(128)S(1)} %shard_map.86.refs_0_, s32[512]{0:T(512)S(1)} %copy-done.2, bf16[48,4096]{1,0:T(8,128)(2,1)S(1)} %collective-permute-done.12.refs_2_, bf16[48,4096]{1,0:T(8,128)(2,1)S(1)} %collective-permute-done.13.refs_3_, bf16[48,4096]{1,0:T(8,128)(2,1)S(1)} %collective-permute-done.14.refs_4_, ...), custom_call_target="tpu_custom_call" | custom-call | flops 2868903936 | bytes 19922944 | tf_op jit(solution)/shard_map/pallas_call | solution.py:213
  42.7 14.3 %all_to_all.5.rows_ref = f32[32,16,128]{2,1,0:T(8,128)S(1)} all-to-all(f32[32,16,128]{2,1,0:T(8,128)S(1)} %bitcast.3), channel_id=1, replica_groups=mesh['vocab'=32,'group'=4] {'vocab'}, dimensions={0} | all-to-all | bytes 524288 | tf_op jit(solution)/shard_map/all_to_all | solution.py:314
  57.1 0.9 %shard_map.90 = (f32[16,64]{1,0:T(8,128)}, f32[1,16]{1,0:T(1,128)}) custom-call(f32[32,16,128]{2,1,0:T(8,128)S(1)} %all_to_all.5.rows_ref), custom_call_target="tpu_custom_call" | custom-call | tf_op jit(solution)/shard_map/pallas_call | solution.py:259
  (7 shorter events, 0.1 us)
Async XLA Ops:
  0.6 9.3 %collective-permute-start = (bf16[16,4096]{1,0:T(8,128)(2,1)}, bf16[16,4096]{1,0:T(8,128)(2,1)S(1)}, u32[]{:S(2)}, u32[]{:S(2)}) collective-permute-start(bf16[16,4096]{1,0:T(8,128)(2,1)} %refs_1_.2), channel_id=1, source_target_pairs={{0,32},{4,12},{8,40},{12,20},{16,48},{20,28},{24,56},{28,4},{32,64... | collective-permute-start | bytes 393224 | tf_op jit(solution)/shard_map/ppermute | solution.py:275
  3.2 8.4 %collective-permute-start.1 = (bf16[16,4096]{1,0:T(8,128)(2,1)}, bf16[16,4096]{1,0:T(8,128)(2,1)S(1)}, u32[]{:S(2)}, u32[]{:S(2)}) collective-permute-start(bf16[16,4096]{1,0:T(8,128)(2,1)} %refs_1_.2), channel_id=1, source_target_pairs={{0,96},{4,28},{8,104},{12,4},{16,112},{20,12},{24,120},{28,20},{32... | collective-permute-start | bytes 393224 | tf_op jit(solution)/shard_map/ppermute | solution.py:275
  5.4 8.7 %collective-permute-start.2 = (bf16[16,4096]{1,0:T(8,128)(2,1)}, bf16[16,4096]{1,0:T(8,128)(2,1)S(1)}, u32[]{:S(2)}, u32[]{:S(2)}) collective-permute-start(bf16[16,4096]{1,0:T(8,128)(2,1)} %refs_1_.2), channel_id=1, source_target_pairs={{0,64},{4,20},{8,72},{12,28},{16,80},{20,4},{24,88},{28,12},{32,96... | collective-permute-start | bytes 393224 | tf_op jit(solution)/shard_map/ppermute | solution.py:275
  6.6 7.6 %collective-permute-start.6 = (bf16[16,4096]{1,0:T(8,128)(2,1)}, bf16[16,4096]{1,0:T(8,128)(2,1)S(1)}, u32[]{:S(2)}, u32[]{:S(2)}) collective-permute-start(bf16[16,4096]{1,0:T(8,128)(2,1)} %refs_1_.2), channel_id=1, source_target_pairs={{0,8},{4,36},{8,16},{12,44},{16,24},{20,52},{24,0},{28,60},{32,40}... | collective-permute-start | bytes 393224 | tf_op jit(solution)/shard_map/ppermute | solution.py:275
  7.8 6.4 %collective-permute-start.7 = (bf16[16,4096]{1,0:T(8,128)(2,1)}, bf16[16,4096]{1,0:T(8,128)(2,1)S(1)}, u32[]{:S(2)}, u32[]{:S(2)}) collective-permute-start(bf16[16,4096]{1,0:T(8,128)(2,1)} %refs_1_.2), channel_id=1, source_target_pairs={{0,24},{4,100},{8,0},{12,108},{16,8},{20,116},{24,16},{28,124},{32... | collective-permute-start | bytes 393224 | tf_op jit(solution)/shard_map/ppermute | solution.py:275
  10.0 5.6 %collective-permute-start.8 = (bf16[16,4096]{1,0:T(8,128)(2,1)}, bf16[16,4096]{1,0:T(8,128)(2,1)S(1)}, u32[]{:S(2)}, u32[]{:S(2)}) collective-permute-start(bf16[16,4096]{1,0:T(8,128)(2,1)} %refs_1_.2), channel_id=1, source_target_pairs={{0,16},{4,68},{8,24},{12,76},{16,0},{20,84},{24,8},{28,92},{32,48}... | collective-permute-start | bytes 393224 | tf_op jit(solution)/shard_map/ppermute | solution.py:275
  11.6 10.0 %collective-permute-start.9 = (bf16[16,4096]{1,0:T(8,128)(2,1)}, bf16[16,4096]{1,0:T(8,128)(2,1)S(1)}, u32[]{:S(2)}, u32[]{:S(2)}) collective-permute-start(bf16[16,4096]{1,0:T(8,128)(2,1)} %refs_1_.2), channel_id=1, source_target_pairs={{0,4},{4,0},{8,12},{12,8},{16,20},{20,16},{24,28},{28,24},{32,36},... | collective-permute-start | bytes 393224 | tf_op jit(solution)/shard_map/ppermute | solution.py:287
  14.1 7.7 %collective-permute-start.10 = (bf16[48,4096]{1,0:T(8,128)(2,1)S(1)}, bf16[48,4096]{1,0:T(8,128)(2,1)S(1)}, u32[]{:S(2)}, u32[]{:S(2)}) collective-permute-start(bf16[48,4096]{1,0:T(8,128)(2,1)S(1)} %constant_dynamic-update-slice_fusion.refs_2_), channel_id=1, source_target_pairs={{0,4},{4,0},{8,12},{12,8},{16,20},{20,16},{24,28},{28,24},{32,36},... | collective-permute-start | bytes 1179656 | tf_op jit(solution)/shard_map/ppermute | solution.py:287
  15.6 6.2 %copy-start = (bf16[16,4096]{1,0:T(8,128)(2,1)S(1)}, bf16[16,4096]{1,0:T(8,128)(2,1)}, u32[]{:S(2)}) copy-start(bf16[16,4096]{1,0:T(8,128)(2,1)} %refs_1_.2) | copy-start | bytes 393220
  15.6 6.2 %copy-start.1 = (s32[512,64]{0,1:T(8,128)S(1)}, s32[512,64]{0,1:T(8,128)}, u32[]{:S(2)}) copy-start(s32[512,64]{0,1:T(8,128)} %param.9) | copy-start | bytes 393220
  15.6 6.2 %collective-permute-start.11 = (bf16[48,4096]{1,0:T(8,128)(2,1)S(1)}, bf16[48,4096]{1,0:T(8,128)(2,1)S(1)}, u32[]{:S(2)}, u32[]{:S(2)}) collective-permute-start(bf16[48,4096]{1,0:T(8,128)(2,1)S(1)} %constant_dynamic-update-slice_fusion.3.refs_3_), channel_id=1, source_target_pairs={{0,4},{4,0},{8,12},{12,8},{16,20},{20,16},{24,28},{28,24},{32,36},... | collective-permute-start | bytes 1179656 | tf_op jit(solution)/shard_map/ppermute | solution.py:287
  18.9 12.6 %collective-permute-start.3 = (bf16[48,4096]{1,0:T(8,128)(2,1)S(1)}, bf16[48,4096]{1,0:T(8,128)(2,1)S(1)}, u32[]{:S(2)}, u32[]{:S(2)}) collective-permute-start(bf16[48,4096]{1,0:T(8,128)(2,1)S(1)} %constant_dynamic-update-slice_fusion.refs_2_), channel_id=1, source_target_pairs={{0,8},{4,36},{8,16},{12,44},{16,24},{20,52},{24,0},{28,60},{32,40}... | collective-permute-start | bytes 1179656 | tf_op jit(solution)/shard_map/ppermute | solution.py:275
  19.2 12.3 %collective-permute-start.4 = (bf16[48,4096]{1,0:T(8,128)(2,1)S(1)}, bf16[48,4096]{1,0:T(8,128)(2,1)S(1)}, u32[]{:S(2)}, u32[]{:S(2)}) collective-permute-start(bf16[48,4096]{1,0:T(8,128)(2,1)S(1)} %constant_dynamic-update-slice_fusion.refs_2_), channel_id=1, source_target_pairs={{0,24},{4,100},{8,0},{12,108},{16,8},{20,116},{24,16},{28,124},{32... | collective-permute-start | bytes 1179656 | tf_op jit(solution)/shard_map/ppermute | solution.py:275
  21.5 10.0 %collective-permute-start.5 = (bf16[48,4096]{1,0:T(8,128)(2,1)S(1)}, bf16[48,4096]{1,0:T(8,128)(2,1)S(1)}, u32[]{:S(2)}, u32[]{:S(2)}) collective-permute-start(bf16[48,4096]{1,0:T(8,128)(2,1)S(1)} %constant_dynamic-update-slice_fusion.refs_2_), channel_id=1, source_target_pairs={{0,16},{4,68},{8,24},{12,76},{16,0},{20,84},{24,8},{28,92},{32,48}... | collective-permute-start | bytes 1179656 | tf_op jit(solution)/shard_map/ppermute | solution.py:275
  21.8 15.9 %copy-start.2 = (s32[512]{0:T(512)S(1)}, s32[512]{0:T(512)}, u32[]{:S(2)}) copy-start(s32[512]{0:T(512)} %refs_1_.3) | copy-start | bytes 6148
  31.5 6.1 %collective-permute-start.12 = (bf16[48,4096]{1,0:T(8,128)(2,1)S(1)}, bf16[48,4096]{1,0:T(8,128)(2,1)S(1)}, u32[]{:S(2)}, u32[]{:S(2)}) collective-permute-start(bf16[48,4096]{1,0:T(8,128)(2,1)S(1)} %collective-permute-done.3.refs_1_), channel_id=1, source_target_pairs={{0,4},{4,0},{8,12},{12,8},{16,20},{20,16},{24,28},{28,24},{32,36},... | collective-permute-start | bytes 1179656 | tf_op jit(solution)/shard_map/ppermute | solution.py:287
  32.7 5.0 %collective-permute-start.13 = (bf16[48,4096]{1,0:T(8,128)(2,1)S(1)}, bf16[48,4096]{1,0:T(8,128)(2,1)S(1)}, u32[]{:S(2)}, u32[]{:S(2)}) collective-permute-start(bf16[48,4096]{1,0:T(8,128)(2,1)S(1)} %collective-permute-done.4.refs_2_), channel_id=1, source_target_pairs={{0,4},{4,0},{8,12},{12,8},{16,20},{20,16},{24,28},{28,24},{32,36},... | collective-permute-start | bytes 1179656 | tf_op jit(solution)/shard_map/ppermute | solution.py:287
  32.8 4.9 %collective-permute-start.14 = (bf16[48,4096]{1,0:T(8,128)(2,1)S(1)}, bf16[48,4096]{1,0:T(8,128)(2,1)S(1)}, u32[]{:S(2)}, u32[]{:S(2)}) collective-permute-start(bf16[48,4096]{1,0:T(8,128)(2,1)S(1)} %collective-permute-done.5.refs_3_), channel_id=1, source_target_pairs={{0,4},{4,0},{8,12},{12,8},{16,20},{20,16},{24,28},{28,24},{32,36},... | collective-permute-start | bytes 1179656 | tf_op jit(solution)/shard_map/ppermute | solution.py:287
where the time goes:
time: 58.1 us; the launch traced here: 58 us
  starting transfers between devices  20.6 us (35%)
  Pallas kernels  20.1 us (35%)
  blocking collectives  14.3 us (25%)
  waiting for transfers between devices  1.39 us (2%)
  between operations  0.8 us (1%)
  other arithmetic  0.7 us (1%)
    pallas_call x3, Pallas kernels, chunk(): pl.pallas_call(functools.partial(chunk_kernel, pieces=len(xs), blocks=mem...  19.2 us
    all_to_all x1, blocking collectives, program(): lax.all_to_all(rows, AXIS, split_axis=0, concat_axis=0, tiled=True)  14.3 us
    ppermute x9, starting transfers between devices, shifts(): received.append(lax.ppermute(value, AXIS, along(k, phase)))  13.1 us
    ppermute x6, starting transfers between devices, swapped(): return lax.ppermute(value, AXIS, swap)  7.46 us
    ppermute x9, waiting for transfers between devices, shifts(): received.append(lax.ppermute(value, AXIS, along(k, phase)))  1.37 us
  transfers between devices with their start and end apart: 15, of which 1 were waited for; matrix products, arithmetic and copies ran while one was open for 1% of the time, Pallas kernels for 24%

commit v1 on v0

--- a/solution.py
+++ b/solution.py
@@ -2,7 +2,6 @@
 
 import jax
 import jax.numpy as jnp
-import numpy as np
 from jax import lax
 from jax.experimental import pallas as pl
 from jax.experimental.pallas import tpu as pltpu
@@ -16,8 +15,9 @@
 TILE = 512
 AXIS = "vocab"
 STEPS = (0, 1, 3, 2)
-AHEAD = 3
-SETTLE_FLOPS = 1 << 34
+COVER_FLOPS = 1 << 35
+EARLY = 2 * RING - 1
+LATE = (RING - 1) ** 2
 
 
 def index_of(x, z, core):
@@ -45,34 +45,36 @@
     )
 
 
-def settle(blocks):
-    def kernel(blocks_ref, out_ref):
-        out_ref[...] = blocks_ref[...]
-
-    vector = pl.BlockSpec(memory_space=pltpu.VMEM)
-    return pl.pallas_call(
-        kernel,
-        out_shape=jax.ShapeDtypeStruct(blocks.shape, blocks.dtype),
-        in_specs=[vector],
-        out_specs=vector,
-        compiler_params=pltpu.CompilerParams(vmem_limit_bytes=1024 * 1024),
-        cost_estimate=pl.CostEstimate(
-            flops=SETTLE_FLOPS, bytes_accessed=1024, transcendentals=0
-        ),
-    )(blocks)
-
-
-def gathered_blocks(mine, arrivals):
-    x, z, c = place_of(mine)
-    at = np.array([(STEPS[second], STEPS[first], other) for second, first, other in arrivals])
-    second, first, other = (jnp.asarray(v, jnp.int32) for v in at.T)
+def table_kernel(out_ref):
+    x, z, c = place_of(lax.axis_index(AXIS))
+    at = lax.broadcasted_iota(jnp.int32, out_ref.shape, 1)
+    late = at - 2 * EARLY
+    one = jnp.ones_like(at)
+    other = jnp.where(at >= EARLY, one, 0) - jnp.where(late >= 0, one, 0) + jnp.where(late >= LATE, one, 0)
+    soon = at - EARLY * other
+    late = late - LATE * other
+    turn = jnp.where(late >= RING - 1, one, 0) + jnp.where(late >= 2 * (RING - 1), one, 0)
+    second = jnp.where(at < 2 * EARLY, jnp.maximum(soon - (RING - 1), 0), 1 + turn)
+    first = jnp.where(soon >= RING, 0, soon)
+    first = jnp.where(at < 2 * EARLY, first, 1 + late - (RING - 1) * turn)
+    first, second = first ^ (first >> 1), second ^ (second >> 1)
     core = c ^ other
     from_x = (x - jnp.where(core == 0, first, second)) & 3
     from_z = (z - jnp.where(core == 0, second, first)) & 3
-    return index_of(from_x, from_z, core)
-
-
-def chunk_kernel(*refs, pieces, blocks, ahead, loads, last):
+    out_ref[...] = index_of(from_x, from_z, core)
+
+
+def table():
+    return pl.pallas_call(
+        table_kernel,
+        out_shape=jax.ShapeDtypeStruct((1, LANES), jnp.int32),
+        out_specs=pl.BlockSpec(memory_space=pltpu.VMEM),
+        compiler_params=pltpu.CompilerParams(vmem_limit_bytes=1024 * 1024),
+        cost_estimate=pl.CostEstimate(flops=COVER_FLOPS, bytes_accessed=1024, transcendentals=0),
+    )()
+
+
+def chunk_kernel(*refs, pieces, blocks, ahead, first, last):
     refs = list(refs)
 
     def take(n):
@@ -84,23 +86,14 @@
         (order_ref,) = take(1)
     x_refs, held_refs = take(pieces), take(ahead)
     weight_ref, index_ref, out_ref = take(3)
-    if loads:
-        source_ref, picks_ref = weight_ref, index_ref
-        weight_ref, index_ref = take(2)
+    if first:
+        picks_ref = index_ref
+        (index_ref,) = take(1)
     x_all, index_here, even, odd, top_ref, sum_ref, found_ref = take(7)
     count = x_all.shape[0]
     width = weight_ref.shape[1]
     edges = [(left, min(left + TILE, width)) for left in range(0, width, TILE)]
-    copies = []
-    if loads:
-        (done,) = take(1)
-        copies = [
-            pltpu.make_async_copy(source_ref.at[:, l:r], weight_ref.at[:, l:r], done.at[t])
-            for t, (l, r) in enumerate(edges)
-        ]
-        for copy in copies[:AHEAD]:
-            copy.start()
-    if loads:
+    if first:
         picks, tokens = picks_ref.shape
         for left in range(0, tokens, LANES):
             some = picks_ref[:, left : left + LANES]
@@ -110,10 +103,10 @@
     for x_ref in x_refs:
         x_all[at : at + x_ref.shape[0], :] = x_ref[...]
         at += x_ref.shape[0]
-    block_rows = index_ref.shape[0] // block_ref.shape[0]
+    block_rows = index_ref.shape[0] // (RING * RING * CORES)
 
     def rows_of(block):
-        return pl.ds(pl.multiple_of(block_ref[block] * block_rows, block_rows), block_rows)
+        return pl.ds(pl.multiple_of(block_ref[0, block] * block_rows, block_rows), block_rows)
 
     start = lax.axis_index(AXIS) * width
     for b, block in enumerate(blocks):
@@ -145,10 +138,6 @@
 
     waiting = None
     for t, (left, right) in enumerate(edges):
-        if copies:
-            copies[t].wait()
-            if t + AHEAD < len(copies):
-                copies[t + AHEAD].start()
         logits = (even, odd)[t % 2]
         logits[:, : right - left] = jnp.dot(
             x_all[...], weight_ref[:, left:right], preferred_element_type=jnp.float32
@@ -186,11 +175,11 @@
         lax.fori_loop(0, out_ref.shape[0] // unroll, move, 0)
 
 
-def chunk(blocks, xs, members, held, weight, index, order=None, loads=False):
+def chunk(blocks, xs, members, held, weight, index, order=None, first=False):
     last = order is not None
     count = sum(x.shape[0] for x in xs)
     depth, width = weight.shape
-    tokens = index.shape[1 if loads else 0]
+    tokens = index.shape[1 if first else 0]
     scalar = pl.BlockSpec(memory_space=pltpu.SMEM)
     vector = pl.BlockSpec(memory_space=pltpu.VMEM)
     rows = pltpu.VMEM((count, LANES), jnp.float32)
@@ -204,10 +193,8 @@
         rows,
         rows,
     ]
-    if loads:
-        out_shape.append(jax.ShapeDtypeStruct((depth, width), weight.dtype))
+    if first:
         out_shape.append(jax.ShapeDtypeStruct((tokens, LANES), jnp.int32))
-        scratch.append(pltpu.SemaphoreType.DMA((pl.cdiv(width, TILE),)))
     if last:
         scratch += [pltpu.VMEM((tokens, LANES), jnp.float32), rows]
     out = pl.pallas_call(
@@ -216,25 +203,22 @@
             pieces=len(xs),
             blocks=members,
             ahead=len(held),
-            loads=loads,
+            first=first,
             last=last,
         ),
         out_shape=out_shape,
         in_specs=[scalar] * (2 if last else 1)
-        + [vector] * (len(xs) + len(held))
-        + [pl.BlockSpec(memory_space=pltpu.HBM) if loads else vector, vector],
+        + [vector] * (len(xs) + len(held) + 2),
         out_specs=[vector] * len(out_shape),
         scratch_shapes=scratch,
-        compiler_params=pltpu.CompilerParams(
-            vmem_limit_bytes=(22 if loads else 16) * 1024 * 1024
-        ),
+        compiler_params=pltpu.CompilerParams(vmem_limit_bytes=12 * 1024 * 1024),
         cost_estimate=pl.CostEstimate(
             flops=2 * count * depth * width,
             bytes_accessed=2 * depth * width,
             transcendentals=count * width,
         ),
     )(blocks, *([order] if last else []), *xs, *held, weight, index)
-    return out if loads else out[0]
+    return out if first else out[0]
 
 
 def combine_kernel(rows_ref, logprobs_ref, log_total_ref):
@@ -278,7 +262,6 @@
 
 def program(hidden_states, head_weight, pick_index, owner_order):
     shard_count = lax.axis_size(AXIS)
-    mine = lax.axis_index(AXIS)
     own_rows = hidden_states.shape[0]
     pick_count = pick_index.shape[1]
     swap = pairs(lambda x, z, c: (x, z, 1 - c))
@@ -286,30 +269,22 @@
     def swapped(value):
         return lax.ppermute(value, AXIS, swap)
 
+    blocks = table()
     own = hidden_states
     line = jnp.concatenate(shifts(own, 0))
     cross = jnp.concatenate(shifts(own, 1))
     rest = shifts(line, 1)
     early = {"own": own, "line": line, "cross": cross}
-    steps = range(1, RING)
-    members = [(0, 0)] + [(0, i) for i in steps] + [(j, 0) for j in steps]
-    late = [(j, i) for j in steps for i in steps]
-    arrivals = [
-        (j, i, other) for group in (members, late) for other in (0, 1) for j, i in group
-    ]
-    blocks = settle(gathered_blocks(mine, arrivals))
     at = list(range(shard_count))
-    cut = 2 * len(members), 2 * len(members) + len(late)
+    cut = 2 * EARLY, 2 * EARLY + LATE
     others = [swapped(v) for v in early.values()]
     xs = [*early.values(), *others]
-    first, weight, index = chunk(
-        blocks, xs, at[: cut[0]], [], head_weight, pick_index.T, loads=True
-    )
+    first, index = chunk(blocks, xs, at[: cut[0]], [], head_weight, pick_index.T, first=True)
     *rest, first = lax.optimization_barrier((*rest, first))
-    second = chunk(blocks, rest, at[cut[0] : cut[1]], [], weight, index)
+    second = chunk(blocks, rest, at[cut[0] : cut[1]], [], head_weight, index)
     others = [swapped(v) for v in rest]
     held = [first, second]
-    rows = chunk(blocks, others, at[cut[1] :], held, weight, index, order=owner_order)
+    rows = chunk(blocks, others, at[cut[1] :], held, head_weight, index, order=owner_order)
     rows = rows.reshape(shard_count, own_rows, LANES)
     received = lax.all_to_all(rows, AXIS, split_axis=0, concat_axis=0, tiled=True)
     return combine(received, pick_count)

time: 58.1 us -> 56.1 us (0.966)
  waiting for transfers between devices: 1.39 us -> 5.08 us
  Pallas kernels: 20.1 us -> 16.7 us
  blocking collectives: 14.3 us -> 12 us
  local copies, waits for them, and re-layouts: 0.08 us -> 1.09 us
  other arithmetic: 0.7 us -> 0.01 us
    ppermute x9, waiting for transfers between devices: 1.37 us -> 5.06 us  [shifts(): received.append(lax.ppermute(value, AXIS, along(k, phase)))]
    pallas_call x3, Pallas kernels: 19.2 us -> 15.8 us  [chunk(): pl.pallas_call(functools.partial(chunk_kernel, pieces=len(xs), blocks=mem...]
    all_to_all x1, blocking collectives: 14.3 us -> 12 us  [program(): lax.all_to_all(rows, AXIS, split_axis=0, concat_axis=0, tiled=True)]
    unnamed x10 -> x20, local copies, waits for them, and re-layouts: 0.06 us -> 1.07 us
    add x1 -> x0, other arithmetic: 0.7 us -> none  [index_of(): return (x * RING + z) * CORES + core]
  transfers between devices with their start and end apart: 15 -> 15, of which waited for: 1 -> 3; matrix products, arithmetic and copies ran while one was open for 1% -> 0% of each run, Pallas kernels for 24% -> 19%
where the time goes in v1:
time: 56.1 us; the launch traced here: 56 us
  starting transfers between devices  20.3 us (36%)
  Pallas kernels  16.7 us (30%)
  blocking collectives  12 us (21%)
  waiting for transfers between devices  5.08 us (9%)
  local copies, waits for them, and re-layouts  1.09 us (2%)
  between operations  0.85 us (2%)
    pallas_call x3, Pallas kernels, chunk(): pl.pallas_call(functools.partial(chunk_kernel, pieces=len(xs), blocks=mem...  15.8 us
    ppermute x9, starting transfers between devices, shifts(): received.append(lax.ppermute(value, AXIS, along(k, phase)))  12.6 us
    all_to_all x1, blocking collectives, program(): lax.all_to_all(rows, AXIS, split_axis=0, concat_axis=0, tiled=True)  12 us
    ppermute x6, starting transfers between devices, swapped(): return lax.ppermute(value, AXIS, swap)  7.65 us
    ppermute x9, waiting for transfers between devices, shifts(): received.append(lax.ppermute(value, AXIS, along(k, phase)))  5.06 us
  transfers between devices with their start and end apart: 15, of which 3 were waited for; matrix products, arithmetic and copies ran while one was open for 0% of the time, Pallas kernels for 19%

profile of v1, /device:TPU:1, one launch (start us, length us, event | category | flops | bytes accessed | tf_op | source)
XLA Modules:
  0.0 56.0 jit_solution(7229743387273876025)
XLA Ops:
  0.6 2.1 %collective-permute-start.6 = (bf16[16,4096]{1,0:T(8,128)(2,1)}, bf16[16,4096]{1,0:T(8,128)(2,1)S(1)}, u32[]{:S(2)}, u32[]{:S(2)}) collective-permute-start(bf16[16,4096]{1,0:T(8,128)(2,1)} %refs_1_.2), channel_id=1, source_target_pairs={{0,8},{4,36},{8,16},{12,44},{16,24},{20,52},{24,0},{28,60},{32,40}... | collective-permute-start | bytes 393224 | tf_op jit(solution)/shard_map/ppermute | solution.py:259
  2.7 2.5 %collective-permute-start.8 = (bf16[16,4096]{1,0:T(8,128)(2,1)}, bf16[16,4096]{1,0:T(8,128)(2,1)S(1)}, u32[]{:S(2)}, u32[]{:S(2)}) collective-permute-start(bf16[16,4096]{1,0:T(8,128)(2,1)} %refs_1_.2), channel_id=1, source_target_pairs={{0,16},{4,68},{8,24},{12,76},{16,0},{20,84},{24,8},{28,92},{32,48}... | collective-permute-start | bytes 393224 | tf_op jit(solution)/shard_map/ppermute | solution.py:259
  5.2 1.2 %collective-permute-start.7 = (bf16[16,4096]{1,0:T(8,128)(2,1)}, bf16[16,4096]{1,0:T(8,128)(2,1)S(1)}, u32[]{:S(2)}, u32[]{:S(2)}) collective-permute-start(bf16[16,4096]{1,0:T(8,128)(2,1)} %refs_1_.2), channel_id=1, source_target_pairs={{0,24},{4,100},{8,0},{12,108},{16,8},{20,116},{24,16},{28,124},{32... | collective-permute-start | bytes 393224 | tf_op jit(solution)/shard_map/ppermute | solution.py:259
  6.3 3.6 %collective-permute-start.2 = (bf16[16,4096]{1,0:T(8,128)(2,1)}, bf16[16,4096]{1,0:T(8,128)(2,1)S(1)}, u32[]{:S(2)}, u32[]{:S(2)}) collective-permute-start(bf16[16,4096]{1,0:T(8,128)(2,1)} %refs_1_.2), channel_id=1, source_target_pairs={{0,64},{4,20},{8,72},{12,28},{16,80},{20,4},{24,88},{28,12},{32,96... | collective-permute-start | bytes 393224 | tf_op jit(solution)/shard_map/ppermute | solution.py:259
  9.9 0.4 collective-permute-start.1
  10.4 0.0 collective-permute-done.6
  10.4 1.0 %collective-permute-start = (bf16[16,4096]{1,0:T(8,128)(2,1)}, bf16[16,4096]{1,0:T(8,128)(2,1)S(1)}, u32[]{:S(2)}, u32[]{:S(2)}) collective-permute-start(bf16[16,4096]{1,0:T(8,128)(2,1)} %refs_1_.2), channel_id=1, source_target_pairs={{0,32},{4,12},{8,40},{12,20},{16,48},{20,28},{24,56},{28,4},{32,64... | collective-permute-start | bytes 393224 | tf_op jit(solution)/shard_map/ppermute | solution.py:259
  11.4 0.0 collective-permute-done.7
  11.4 2.4 %collective-permute-start.9 = (bf16[16,4096]{1,0:T(8,128)(2,1)}, bf16[16,4096]{1,0:T(8,128)(2,1)S(1)}, u32[]{:S(2)}, u32[]{:S(2)}) collective-permute-start(bf16[16,4096]{1,0:T(8,128)(2,1)} %refs_1_.2), channel_id=1, source_target_pairs={{0,4},{4,0},{8,12},{12,8},{16,20},{20,16},{24,28},{28,24},{32,36},... | collective-permute-start | bytes 393224 | tf_op jit(solution)/shard_map/ppermute | solution.py:270
  13.9 0.0 collective-permute-done.8
  13.9 0.1 collective-permute-start.11
  14.0 1.6 %collective-permute-done = bf16[16,4096]{1,0:T(8,128)(2,1)S(1)} collective-permute-done((bf16[16,4096]{1,0:T(8,128)(2,1)}, bf16[16,4096]{1,0:T(8,128)(2,1)S(1)}, u32[]{:S(2)}, u32[]{:S(2)}) %collective-permute-start) | collective-permute-done | bytes 131104 | tf_op jit(solution)/shard_map/ppermute | solution.py:259
  15.6 0.0 collective-permute-done.1
  15.6 0.0 collective-permute-done.2
  15.7 0.0 slice-start
  15.7 0.0 slice-start.1
  15.7 0.0 slice-start.2
  15.7 0.0 slice-start.3
  15.7 0.0 slice-start.4
  15.7 0.0 copy-start
  15.7 0.0 copy-start.1
  15.8 3.7 %collective-permute-start.10 = (bf16[48,4096]{1,0:T(8,128)(2,1)S(1)}, bf16[48,4096]{1,0:T(8,128)(2,1)S(1)}, u32[]{:S(2)}, u32[]{:S(2)}) collective-permute-start(bf16[48,4096]{1,0:T(8,128)(2,1)S(1)} %constant_dynamic-update-slice_fusion.refs_2_), channel_id=1, source_target_pairs={{0,4},{4,0},{8,12},{12,8},{16,20},{20,16},{24,28},{28,24},{32,36},... | collective-permute-start | bytes 1179656 | tf_op jit(solution)/shard_map/ppermute | solution.py:270
  19.5 0.4 collective-permute-start.5
  19.9 1.5 %collective-permute-start.4 = (bf16[48,4096]{1,0:T(8,128)(2,1)S(1)}, bf16[48,4096]{1,0:T(8,128)(2,1)S(1)}, u32[]{:S(2)}, u32[]{:S(2)}) collective-permute-start(bf16[48,4096]{1,0:T(8,128)(2,1)S(1)} %constant_dynamic-update-slice_fusion.refs_2_), channel_id=1, source_target_pairs={{0,24},{4,100},{8,0},{12,108},{16,8},{20,116},{24,16},{28,124},{32... | collective-permute-start | bytes 1179656 | tf_op jit(solution)/shard_map/ppermute | solution.py:259
  21.4 0.0 collective-permute-done.9.refs_4_
  21.4 0.0 collective-permute-start.3
  21.4 0.0 collective-permute-done.11.refs_6_
  21.4 0.0 collective-permute-done.10.refs_5_
  21.4 0.0 slice-done
  21.4 0.0 slice-done.1
  21.4 0.0 slice-done.2
  21.4 0.1 slice-done.3
  21.5 0.9 %slice-done.4 = s8[3145728]{0:T(1024)(128)(4,1)S(1)} async-done(((s8[19922944]{0:T(1024)(128)(4,1)}), s8[3145728]{0:T(1024)(128)(4,1)S(1)}, s32[]{:S(2)}) %slice-start.4) | async-done | bytes 3145752
  22.4 0.0 copy-done
  22.4 6.3 %shard_map.60 = (f32[224,128]{1,0:T(8,128)S(1)}, s32[512,128]{1,0:T(8,128)S(1)}) custom-call(s32[1,128]{1,0:T(1,128)S(1)} %shard_map.59.refs_0_, bf16[16,4096]{1,0:T(8,128)(2,1)S(1)} %copy-done, bf16[48,4096]{1,0:T(8,128)(2,1)S(1)} %constant_dynamic-update-slice_fusion.refs_2_, bf16[48,4096]{1,0:T(8,128)(2,1)S(1)} %constant_dynamic-update-slice_fusion.3.refs_3_, ...), custom_call_target="tpu_custom_call" | custom-call | flops 4462739456 | bytes 19922944 | tf_op jit(solution)/shard_map/pallas_call | solution.py:200
  28.8 0.0 collective-permute-done.5.refs_3_
  28.8 1.1 %collective-permute-done.4.refs_2_ = bf16[48,4096]{1,0:T(8,128)(2,1)S(1)} collective-permute-done((bf16[48,4096]{1,0:T(8,128)(2,1)S(1)}, bf16[48,4096]{1,0:T(8,128)(2,1)S(1)}, u32[]{:S(2)}, u32[]{:S(2)}) %collective-permute-start.4) | collective-permute-done | bytes 393248 | tf_op jit(solution)/shard_map/ppermute | solution.py:259
  29.9 2.4 %collective-permute-done.3.refs_1_ = bf16[48,4096]{1,0:T(8,128)(2,1)S(1)} collective-permute-done((bf16[48,4096]{1,0:T(8,128)(2,1)S(1)}, bf16[48,4096]{1,0:T(8,128)(2,1)S(1)}, u32[]{:S(2)}, u32[]{:S(2)}) %collective-permute-start.3) | collective-permute-done | bytes 393248 | tf_op jit(solution)/shard_map/ppermute | solution.py:259
  32.2 0.9 %collective-permute-start.12 = (bf16[48,4096]{1,0:T(8,128)(2,1)S(1)}, bf16[48,4096]{1,0:T(8,128)(2,1)S(1)}, u32[]{:S(2)}, u32[]{:S(2)}) collective-permute-start(bf16[48,4096]{1,0:T(8,128)(2,1)S(1)} %collective-permute-done.3.refs_1_), channel_id=1, source_target_pairs={{0,4},{4,0},{8,12},{12,8},{16,20},{20,16},{24,28},{28,24},{32,36},... | collective-permute-start | bytes 1179656 | tf_op jit(solution)/shard_map/ppermute | solution.py:270
  33.1 0.0 collective-permute-start.13
  33.1 0.5 collective-permute-start.14
  33.6 4.4 %shard_map.61.refs_6_ = f32[144,128]{1,0:T(8,128)S(1)} custom-call(s32[1,128]{1,0:T(1,128)S(1)} %shard_map.59.refs_0_, bf16[48,4096]{1,0:T(8,128)(2,1)S(1)} %collective-permute-done.3.refs_1_, bf16[48,4096]{1,0:T(8,128)(2,1)S(1)} %collective-permute-done.4.refs_2_, bf16[48,4096]{1,0:T(8,128)(2,1)S(1)} %collective-permute-done.5.refs_3_, ...), custom_call_target="tpu_custom_call" | custom-call | flops 2868903936 | bytes 19922944 | tf_op jit(solution)/shard_map/pallas_call | solution.py:200
  38.1 0.0 collective-permute-done.12.refs_2_
  38.1 0.0 collective-permute-done.13.refs_3_
  38.1 0.0 collective-permute-done.14.refs_4_
  38.1 5.0 %shard_map.62 = f32[512,128]{1,0:T(8,128)S(1)} custom-call(s32[1,128]{1,0:T(1,128)S(1)} %shard_map.59.refs_0_, s32[512]{0:T(512)S(1)} %copy-done.2, bf16[48,4096]{1,0:T(8,128)(2,1)S(1)} %collective-permute-done.12.refs_2_, bf16[48,4096]{1,0:T(8,128)(2,1)S(1)} %collective-permute-done.13.refs_3_, bf16[48,4096]{1,0:T(8,128)(2,1)S(1)} %collective-permute-done.14.refs_4_, ...), custom_call_target="tpu_custom_call" | custom-call | flops 2868903936 | bytes 19922944 | tf_op jit(solution)/shard_map/pallas_call | solution.py:200
  43.1 12.0 %all_to_all.5.rows_ref = f32[32,16,128]{2,1,0:T(8,128)S(1)} all-to-all(f32[32,16,128]{2,1,0:T(8,128)S(1)} %bitcast.5), channel_id=1, replica_groups=mesh['vocab'=32,'group'=4] {'vocab'}, dimensions={0} | all-to-all | bytes 524288 | tf_op jit(solution)/shard_map/all_to_all | solution.py:289
  55.1 0.9 %shard_map.63 = (f32[16,64]{1,0:T(8,128)}, f32[1,16]{1,0:T(1,128)}) custom-call(f32[32,16,128]{2,1,0:T(8,128)S(1)} %all_to_all.5.rows_ref), custom_call_target="tpu_custom_call" | custom-call | tf_op jit(solution)/shard_map/pallas_call | solution.py:243
  (11 shorter events, 0.1 us)
Async XLA Ops:
  0.6 9.7 %collective-permute-start.6 = (bf16[16,4096]{1,0:T(8,128)(2,1)}, bf16[16,4096]{1,0:T(8,128)(2,1)S(1)}, u32[]{:S(2)}, u32[]{:S(2)}) collective-permute-start(bf16[16,4096]{1,0:T(8,128)(2,1)} %refs_1_.2), channel_id=1, source_target_pairs={{0,8},{4,36},{8,16},{12,44},{16,24},{20,52},{24,0},{28,60},{32,40}... | collective-permute-start | bytes 393224 | tf_op jit(solution)/shard_map/ppermute | solution.py:259
  2.7 11.1 %collective-permute-start.8 = (bf16[16,4096]{1,0:T(8,128)(2,1)}, bf16[16,4096]{1,0:T(8,128)(2,1)S(1)}, u32[]{:S(2)}, u32[]{:S(2)}) collective-permute-start(bf16[16,4096]{1,0:T(8,128)(2,1)} %refs_1_.2), channel_id=1, source_target_pairs={{0,16},{4,68},{8,24},{12,76},{16,0},{20,84},{24,8},{28,92},{32,48}... | collective-permute-start | bytes 393224 | tf_op jit(solution)/shard_map/ppermute | solution.py:259
  5.2 6.2 %collective-permute-start.7 = (bf16[16,4096]{1,0:T(8,128)(2,1)}, bf16[16,4096]{1,0:T(8,128)(2,1)S(1)}, u32[]{:S(2)}, u32[]{:S(2)}) collective-permute-start(bf16[16,4096]{1,0:T(8,128)(2,1)} %refs_1_.2), channel_id=1, source_target_pairs={{0,24},{4,100},{8,0},{12,108},{16,8},{20,116},{24,16},{28,124},{32... | collective-permute-start | bytes 393224 | tf_op jit(solution)/shard_map/ppermute | solution.py:259
  6.3 9.3 %collective-permute-start.2 = (bf16[16,4096]{1,0:T(8,128)(2,1)}, bf16[16,4096]{1,0:T(8,128)(2,1)S(1)}, u32[]{:S(2)}, u32[]{:S(2)}) collective-permute-start(bf16[16,4096]{1,0:T(8,128)(2,1)} %refs_1_.2), channel_id=1, source_target_pairs={{0,64},{4,20},{8,72},{12,28},{16,80},{20,4},{24,88},{28,12},{32,96... | collective-permute-start | bytes 393224 | tf_op jit(solution)/shard_map/ppermute | solution.py:259
  9.9 5.7 %collective-permute-start.1 = (bf16[16,4096]{1,0:T(8,128)(2,1)}, bf16[16,4096]{1,0:T(8,128)(2,1)S(1)}, u32[]{:S(2)}, u32[]{:S(2)}) collective-permute-start(bf16[16,4096]{1,0:T(8,128)(2,1)} %refs_1_.2), channel_id=1, source_target_pairs={{0,96},{4,28},{8,104},{12,4},{16,112},{20,12},{24,120},{28,20},{32... | collective-permute-start | bytes 393224 | tf_op jit(solution)/shard_map/ppermute | solution.py:259
  10.4 5.2 %collective-permute-start = (bf16[16,4096]{1,0:T(8,128)(2,1)}, bf16[16,4096]{1,0:T(8,128)(2,1)S(1)}, u32[]{:S(2)}, u32[]{:S(2)}) collective-permute-start(bf16[16,4096]{1,0:T(8,128)(2,1)} %refs_1_.2), channel_id=1, source_target_pairs={{0,32},{4,12},{8,40},{12,20},{16,48},{20,28},{24,56},{28,4},{32,64... | collective-permute-start | bytes 393224 | tf_op jit(solution)/shard_map/ppermute | solution.py:259
  11.4 10.0 %collective-permute-start.9 = (bf16[16,4096]{1,0:T(8,128)(2,1)}, bf16[16,4096]{1,0:T(8,128)(2,1)S(1)}, u32[]{:S(2)}, u32[]{:S(2)}) collective-permute-start(bf16[16,4096]{1,0:T(8,128)(2,1)} %refs_1_.2), channel_id=1, source_target_pairs={{0,4},{4,0},{8,12},{12,8},{16,20},{20,16},{24,28},{28,24},{32,36},... | collective-permute-start | bytes 393224 | tf_op jit(solution)/shard_map/ppermute | solution.py:270
  13.9 7.5 %collective-permute-start.11 = (bf16[48,4096]{1,0:T(8,128)(2,1)S(1)}, bf16[48,4096]{1,0:T(8,128)(2,1)S(1)}, u32[]{:S(2)}, u32[]{:S(2)}) collective-permute-start(bf16[48,4096]{1,0:T(8,128)(2,1)S(1)} %constant_dynamic-update-slice_fusion.3.refs_3_), channel_id=1, source_target_pairs={{0,4},{4,0},{8,12},{12,8},{16,20},{20,16},{24,28},{28,24},{32,36},... | collective-permute-start | bytes 1179656 | tf_op jit(solution)/shard_map/ppermute | solution.py:270
  15.7 5.7 %slice-start = ((s8[19922944]{0:T(1024)(128)(4,1)}), s8[4194304]{0:T(1024)(128)(4,1)S(1)}, s32[]{:S(2)}) async-start(s8[19922944]{0:T(1024)(128)(4,1)} %bitcast.3), calls=%async_computation.1 | async-start | bytes 8388608
  15.7 5.7 %slice-start.1 = ((s8[19922944]{0:T(1024)(128)(4,1)}), s8[4194304]{0:T(1024)(128)(4,1)S(1)}, s32[]{:S(2)}) async-start(s8[19922944]{0:T(1024)(128)(4,1)} %bitcast.3), calls=%async_computation.2 | async-start | bytes 8388608
  15.7 5.7 %slice-start.2 = ((s8[19922944]{0:T(1024)(128)(4,1)}), s8[4194304]{0:T(1024)(128)(4,1)S(1)}, s32[]{:S(2)}) async-start(s8[19922944]{0:T(1024)(128)(4,1)} %bitcast.3), calls=%async_computation.3 | async-start | bytes 8388608
  15.7 5.8 %slice-start.3 = ((s8[19922944]{0:T(1024)(128)(4,1)}), s8[4194304]{0:T(1024)(128)(4,1)S(1)}, s32[]{:S(2)}) async-start(s8[19922944]{0:T(1024)(128)(4,1)} %bitcast.3), calls=%async_computation.4 | async-start | bytes 8388608
  15.7 6.7 %slice-start.4 = ((s8[19922944]{0:T(1024)(128)(4,1)}), s8[3145728]{0:T(1024)(128)(4,1)S(1)}, s32[]{:S(2)}) async-start(s8[19922944]{0:T(1024)(128)(4,1)} %bitcast.3), calls=%async_computation.5 | async-start | bytes 6291456
  15.7 6.7 %copy-start = (bf16[16,4096]{1,0:T(8,128)(2,1)S(1)}, bf16[16,4096]{1,0:T(8,128)(2,1)}, u32[]{:S(2)}) copy-start(bf16[16,4096]{1,0:T(8,128)(2,1)} %refs_1_.2) | copy-start | bytes 393220
  15.7 6.7 %copy-start.1 = (s32[512,64]{0,1:T(8,128)S(1)}, s32[512,64]{0,1:T(8,128)}, u32[]{:S(2)}) copy-start(s32[512,64]{0,1:T(8,128)} %param.6) | copy-start | bytes 393220
  15.8 5.6 %collective-permute-start.10 = (bf16[48,4096]{1,0:T(8,128)(2,1)S(1)}, bf16[48,4096]{1,0:T(8,128)(2,1)S(1)}, u32[]{:S(2)}, u32[]{:S(2)}) collective-permute-start(bf16[48,4096]{1,0:T(8,128)(2,1)S(1)} %constant_dynamic-update-slice_fusion.refs_2_), channel_id=1, source_target_pairs={{0,4},{4,0},{8,12},{12,8},{16,20},{20,16},{24,28},{28,24},{32,36},... | collective-permute-start | bytes 1179656 | tf_op jit(solution)/shard_map/ppermute | solution.py:270
  19.5 9.3 %collective-permute-start.5 = (bf16[48,4096]{1,0:T(8,128)(2,1)S(1)}, bf16[48,4096]{1,0:T(8,128)(2,1)S(1)}, u32[]{:S(2)}, u32[]{:S(2)}) collective-permute-start(bf16[48,4096]{1,0:T(8,128)(2,1)S(1)} %constant_dynamic-update-slice_fusion.refs_2_), channel_id=1, source_target_pairs={{0,16},{4,68},{8,24},{12,76},{16,0},{20,84},{24,8},{28,92},{32,48}... | collective-permute-start | bytes 1179656 | tf_op jit(solution)/shard_map/ppermute | solution.py:259
  19.9 10.0 %collective-permute-start.4 = (bf16[48,4096]{1,0:T(8,128)(2,1)S(1)}, bf16[48,4096]{1,0:T(8,128)(2,1)S(1)}, u32[]{:S(2)}, u32[]{:S(2)}) collective-permute-start(bf16[48,4096]{1,0:T(8,128)(2,1)S(1)} %constant_dynamic-update-slice_fusion.refs_2_), channel_id=1, source_target_pairs={{0,24},{4,100},{8,0},{12,108},{16,8},{20,116},{24,16},{28,124},{32... | collective-permute-start | bytes 1179656 | tf_op jit(solution)/shard_map/ppermute | solution.py:259
  21.4 10.8 %collective-permute-start.3 = (bf16[48,4096]{1,0:T(8,128)(2,1)S(1)}, bf16[48,4096]{1,0:T(8,128)(2,1)S(1)}, u32[]{:S(2)}, u32[]{:S(2)}) collective-permute-start(bf16[48,4096]{1,0:T(8,128)(2,1)S(1)} %constant_dynamic-update-slice_fusion.refs_2_), channel_id=1, source_target_pairs={{0,8},{4,36},{8,16},{12,44},{16,24},{20,52},{24,0},{28,60},{32,40}... | collective-permute-start | bytes 1179656 | tf_op jit(solution)/shard_map/ppermute | solution.py:259
  22.4 15.7 %copy-start.2 = (s32[512]{0:T(512)S(1)}, s32[512]{0:T(512)}, u32[]{:S(2)}) copy-start(s32[512]{0:T(512)} %refs_1_.3) | copy-start | bytes 6148
  32.2 5.8 %collective-permute-start.12 = (bf16[48,4096]{1,0:T(8,128)(2,1)S(1)}, bf16[48,4096]{1,0:T(8,128)(2,1)S(1)}, u32[]{:S(2)}, u32[]{:S(2)}) collective-permute-start(bf16[48,4096]{1,0:T(8,128)(2,1)S(1)} %collective-permute-done.3.refs_1_), channel_id=1, source_target_pairs={{0,4},{4,0},{8,12},{12,8},{16,20},{20,16},{24,28},{28,24},{32,36},... | collective-permute-start | bytes 1179656 | tf_op jit(solution)/shard_map/ppermute | solution.py:270
  33.1 5.0 %collective-permute-start.13 = (bf16[48,4096]{1,0:T(8,128)(2,1)S(1)}, bf16[48,4096]{1,0:T(8,128)(2,1)S(1)}, u32[]{:S(2)}, u32[]{:S(2)}) collective-permute-start(bf16[48,4096]{1,0:T(8,128)(2,1)S(1)} %collective-permute-done.4.refs_2_), channel_id=1, source_target_pairs={{0,4},{4,0},{8,12},{12,8},{16,20},{20,16},{24,28},{28,24},{32,36},... | collective-permute-start | bytes 1179656 | tf_op jit(solution)/shard_map/ppermute | solution.py:270
  33.1 5.0 %collective-permute-start.14 = (bf16[48,4096]{1,0:T(8,128)(2,1)S(1)}, bf16[48,4096]{1,0:T(8,128)(2,1)S(1)}, u32[]{:S(2)}, u32[]{:S(2)}) collective-permute-start(bf16[48,4096]{1,0:T(8,128)(2,1)S(1)} %collective-permute-done.5.refs_3_), channel_id=1, source_target_pairs={{0,4},{4,0},{8,12},{12,8},{16,20},{20,16},{24,28},{28,24},{32,36},... | collective-permute-start | bytes 1179656 | tf_op jit(solution)/shard_map/ppermute | solution.py:270

commit v2 on v1

--- a/solution.py
+++ b/solution.py
@@ -16,8 +16,6 @@
 AXIS = "vocab"
 STEPS = (0, 1, 3, 2)
 COVER_FLOPS = 1 << 35
-EARLY = 2 * RING - 1
-LATE = (RING - 1) ** 2
 
 
 def index_of(x, z, core):
@@ -45,19 +43,26 @@
     )
 
 
+def arrivals():
+    steps = range(1, RING)
+    early = [(0, 0)] + [(0, i) for i in steps] + [(j, 0) for j in steps]
+    late = [(j, i) for j in steps for i in steps]
+    near = RING - 1 << 1
+    return [
+        [(*b, other) for other in range(CORES) for b in early],
+        [(*b, 0) for b in late[:near]],
+        [(*b, 0) for b in late[near:]] + [(*b, 1) for b in late],
+    ]
+
+
 def table_kernel(out_ref):
     x, z, c = place_of(lax.axis_index(AXIS))
     at = lax.broadcasted_iota(jnp.int32, out_ref.shape, 1)
-    late = at - 2 * EARLY
-    one = jnp.ones_like(at)
-    other = jnp.where(at >= EARLY, one, 0) - jnp.where(late >= 0, one, 0) + jnp.where(late >= LATE, one, 0)
-    soon = at - EARLY * other
-    late = late - LATE * other
-    turn = jnp.where(late >= RING - 1, one, 0) + jnp.where(late >= 2 * (RING - 1), one, 0)
-    second = jnp.where(at < 2 * EARLY, jnp.maximum(soon - (RING - 1), 0), 1 + turn)
-    first = jnp.where(soon >= RING, 0, soon)
-    first = jnp.where(at < 2 * EARLY, first, 1 + late - (RING - 1) * turn)
-    first, second = first ^ (first >> 1), second ^ (second >> 1)
+    second = first = other = jnp.zeros_like(at)
+    for n, (j, i, swapped) in enumerate(b for part in arrivals() for b in part):
+        second = jnp.where(at == n, STEPS[j], second)
+        first = jnp.where(at == n, STEPS[i], first)
+        other = jnp.where(at == n, swapped, other)
     core = c ^ other
     from_x = (x - jnp.where(core == 0, first, second)) & 3
     from_z = (z - jnp.where(core == 0, second, first)) & 3
@@ -92,7 +97,8 @@
     x_all, index_here, even, odd, top_ref, sum_ref, found_ref = take(7)
     count = x_all.shape[0]
     width = weight_ref.shape[1]
-    edges = [(left, min(left + TILE, width)) for left in range(0, width, TILE)]
+    cuts = [0, width % TILE, *range(width % TILE + TILE, width, TILE), width - TILE // 2, width]
+    edges = [(left, right) for left, right in zip(cuts, cuts[1:]) if left < right]
     if first:
         picks, tokens = picks_ref.shape
         for left in range(0, tokens, LANES):
@@ -276,15 +282,19 @@
     rest = shifts(line, 1)
     early = {"own": own, "line": line, "cross": cross}
     at = list(range(shard_count))
-    cut = 2 * EARLY, 2 * EARLY + LATE
+    sizes = [len(part) for part in arrivals()]
+    cut = sizes[0], sizes[0] + sizes[1]
     others = [swapped(v) for v in early.values()]
     xs = [*early.values(), *others]
     first, index = chunk(blocks, xs, at[: cut[0]], [], head_weight, pick_index.T, first=True)
-    *rest, first = lax.optimization_barrier((*rest, first))
-    second = chunk(blocks, rest, at[cut[0] : cut[1]], [], head_weight, index)
-    others = [swapped(v) for v in rest]
+    *near, far = rest
+    *near, first = lax.optimization_barrier((*near, first))
+    others = [swapped(v) for v in near]
+    second = chunk(blocks, near, at[cut[0] : cut[1]], [], head_weight, index)
+    far, second = lax.optimization_barrier((far, second))
+    xs = [far, *others, swapped(far)]
     held = [first, second]
-    rows = chunk(blocks, others, at[cut[1] :], held, head_weight, index, order=owner_order)
+    rows = chunk(blocks, xs, at[cut[1] :], held, head_weight, index, order=owner_order)
     rows = rows.reshape(shard_count, own_rows, LANES)
     received = lax.all_to_all(rows, AXIS, split_axis=0, concat_axis=0, tiled=True)
     return combine(received, pick_count)

time: 56.1 us -> 58.4 us (1.041)
  waiting for transfers between devices: 5.08 us -> 6.16 us
  Pallas kernels: 16.7 us -> 17.7 us
    ppermute x6, waiting for transfers between devices: 0.02 us -> 1.36 us  [swapped(): return lax.ppermute(value, AXIS, swap)]
    pallas_call x3, Pallas kernels: 15.8 us -> 16.8 us  [chunk(): pl.pallas_call(functools.partial(chunk_kernel, pieces=len(xs), blocks=mem...]
  transfers between devices with their start and end apart: 15 -> 15, of which waited for: 3 -> 3; matrix products, arithmetic and copies ran while one was open for 0% -> 0% of each run, Pallas kernels for 19% -> 18%
where the time goes in v2:
time: 58.4 us; the launch traced here: 58.3 us
  starting transfers between devices  20.3 us (35%)
  Pallas kernels  17.7 us (30%)
  blocking collectives  12.1 us (21%)
  waiting for transfers between devices  6.16 us (11%)
  local copies, waits for them, and re-layouts  1.16 us (2%)
  between operations  0.83 us (1%)
    pallas_call x3, Pallas kernels, chunk(): pl.pallas_call(functools.partial(chunk_kernel, pieces=len(xs), blocks=mem...  16.8 us
    ppermute x9, starting transfers between devices, shifts(): received.append(lax.ppermute(value, AXIS, along(k, phase)))  12.6 us
    all_to_all x1, blocking collectives, program(): lax.all_to_all(rows, AXIS, split_axis=0, concat_axis=0, tiled=True)  12.1 us
    ppermute x6, starting transfers between devices, swapped(): return lax.ppermute(value, AXIS, swap)  7.74 us
    ppermute x9, waiting for transfers between devices, shifts(): received.append(lax.ppermute(value, AXIS, along(k, phase)))  4.8 us
    ppermute x6, waiting for transfers between devices, swapped(): return lax.ppermute(value, AXIS, swap)  1.36 us
  transfers between devices with their start and end apart: 15, of which 3 were waited for; matrix products, arithmetic and copies ran while one was open for 0% of the time, Pallas kernels for 18%

profile of v2, /device:TPU:1, one launch (start us, length us, event | category | flops | bytes accessed | tf_op | source)
XLA Modules:
  0.0 58.3 jit_solution(18256578587256052753)
XLA Ops:
  0.6 2.1 %collective-permute-start.6 = (bf16[16,4096]{1,0:T(8,128)(2,1)}, bf16[16,4096]{1,0:T(8,128)(2,1)S(1)}, u32[]{:S(2)}, u32[]{:S(2)}) collective-permute-start(bf16[16,4096]{1,0:T(8,128)(2,1)} %refs_1_.2), channel_id=1, source_target_pairs={{0,8},{4,36},{8,16},{12,44},{16,24},{20,52},{24,0},{28,60},{32,40}... | collective-permute-start | bytes 393224 | tf_op jit(solution)/shard_map/ppermute | solution.py:265
  2.7 2.5 %collective-permute-start.8 = (bf16[16,4096]{1,0:T(8,128)(2,1)}, bf16[16,4096]{1,0:T(8,128)(2,1)S(1)}, u32[]{:S(2)}, u32[]{:S(2)}) collective-permute-start(bf16[16,4096]{1,0:T(8,128)(2,1)} %refs_1_.2), channel_id=1, source_target_pairs={{0,16},{4,68},{8,24},{12,76},{16,0},{20,84},{24,8},{28,92},{32,48}... | collective-permute-start | bytes 393224 | tf_op jit(solution)/shard_map/ppermute | solution.py:265
  5.2 1.2 %collective-permute-start.7 = (bf16[16,4096]{1,0:T(8,128)(2,1)}, bf16[16,4096]{1,0:T(8,128)(2,1)S(1)}, u32[]{:S(2)}, u32[]{:S(2)}) collective-permute-start(bf16[16,4096]{1,0:T(8,128)(2,1)} %refs_1_.2), channel_id=1, source_target_pairs={{0,24},{4,100},{8,0},{12,108},{16,8},{20,116},{24,16},{28,124},{32... | collective-permute-start | bytes 393224 | tf_op jit(solution)/shard_map/ppermute | solution.py:265
  6.3 3.6 %collective-permute-start.2 = (bf16[16,4096]{1,0:T(8,128)(2,1)}, bf16[16,4096]{1,0:T(8,128)(2,1)S(1)}, u32[]{:S(2)}, u32[]{:S(2)}) collective-permute-start(bf16[16,4096]{1,0:T(8,128)(2,1)} %refs_1_.2), channel_id=1, source_target_pairs={{0,64},{4,20},{8,72},{12,28},{16,80},{20,4},{24,88},{28,12},{32,96... | collective-permute-start | bytes 393224 | tf_op jit(solution)/shard_map/ppermute | solution.py:265
  9.9 0.4 collective-permute-start.1
  10.4 0.0 collective-permute-done.6
  10.4 1.0 %collective-permute-start = (bf16[16,4096]{1,0:T(8,128)(2,1)}, bf16[16,4096]{1,0:T(8,128)(2,1)S(1)}, u32[]{:S(2)}, u32[]{:S(2)}) collective-permute-start(bf16[16,4096]{1,0:T(8,128)(2,1)} %refs_1_.2), channel_id=1, source_target_pairs={{0,32},{4,12},{8,40},{12,20},{16,48},{20,28},{24,56},{28,4},{32,64... | collective-permute-start | bytes 393224 | tf_op jit(solution)/shard_map/ppermute | solution.py:265
  11.4 0.0 collective-permute-done.7
  11.4 2.4 %collective-permute-start.9 = (bf16[16,4096]{1,0:T(8,128)(2,1)}, bf16[16,4096]{1,0:T(8,128)(2,1)S(1)}, u32[]{:S(2)}, u32[]{:S(2)}) collective-permute-start(bf16[16,4096]{1,0:T(8,128)(2,1)} %refs_1_.2), channel_id=1, source_target_pairs={{0,4},{4,0},{8,12},{12,8},{16,20},{20,16},{24,28},{28,24},{32,36},... | collective-permute-start | bytes 393224 | tf_op jit(solution)/shard_map/ppermute | solution.py:276
  13.9 0.0 collective-permute-done.8
  13.9 0.1 collective-permute-start.11
  14.0 1.6 %collective-permute-done = bf16[16,4096]{1,0:T(8,128)(2,1)S(1)} collective-permute-done((bf16[16,4096]{1,0:T(8,128)(2,1)}, bf16[16,4096]{1,0:T(8,128)(2,1)S(1)}, u32[]{:S(2)}, u32[]{:S(2)}) %collective-permute-start) | collective-permute-done | bytes 131104 | tf_op jit(solution)/shard_map/ppermute | solution.py:265
  15.6 0.0 collective-permute-done.1
  15.6 0.0 collective-permute-done.2
  15.7 0.0 slice-start
  15.7 0.0 slice-start.1
  15.7 0.0 slice-start.2
  15.7 0.0 slice-start.3
  15.7 0.0 slice-start.4
  15.7 0.0 copy-start
  15.7 0.0 copy-start.1
  15.8 3.7 %collective-permute-start.10 = (bf16[48,4096]{1,0:T(8,128)(2,1)S(1)}, bf16[48,4096]{1,0:T(8,128)(2,1)S(1)}, u32[]{:S(2)}, u32[]{:S(2)}) collective-permute-start(bf16[48,4096]{1,0:T(8,128)(2,1)S(1)} %constant_dynamic-update-slice_fusion.refs_2_), channel_id=1, source_target_pairs={{0,4},{4,0},{8,12},{12,8},{16,20},{20,16},{24,28},{28,24},{32,36},... | collective-permute-start | bytes 1179656 | tf_op jit(solution)/shard_map/ppermute | solution.py:276
  19.5 0.1 collective-permute-start.5
  19.6 1.5 %collective-permute-start.4 = (bf16[48,4096]{1,0:T(8,128)(2,1)S(1)}, bf16[48,4096]{1,0:T(8,128)(2,1)S(1)}, u32[]{:S(2)}, u32[]{:S(2)}) collective-permute-start(bf16[48,4096]{1,0:T(8,128)(2,1)S(1)} %constant_dynamic-update-slice_fusion.refs_2_), channel_id=1, source_target_pairs={{0,8},{4,36},{8,16},{12,44},{16,24},{20,52},{24,0},{28,60},{32,40}... | collective-permute-start | bytes 1179656 | tf_op jit(solution)/shard_map/ppermute | solution.py:265
  21.1 0.0 collective-permute-done.9.refs_4_
  21.1 0.3 collective-permute-start.3
  21.3 0.0 collective-permute-done.11.refs_6_
  21.3 0.0 collective-permute-done.10.refs_5_
  21.3 0.0 slice-done
  21.3 0.0 slice-done.1
  21.4 0.0 slice-done.2
  21.4 0.2 slice-done.3
  21.5 0.9 %slice-done.4 = s8[3145728]{0:T(1024)(128)(4,1)S(1)} async-done(((s8[19922944]{0:T(1024)(128)(4,1)}), s8[3145728]{0:T(1024)(128)(4,1)S(1)}, s32[]{:S(2)}) %slice-start.4) | async-done | bytes 3145752
  22.4 0.0 copy-done
  22.4 6.4 %shard_map.60 = (f32[224,128]{1,0:T(8,128)S(1)}, s32[512,128]{1,0:T(8,128)S(1)}) custom-call(s32[1,128]{1,0:T(1,128)S(1)} %shard_map.59.refs_0_, bf16[16,4096]{1,0:T(8,128)(2,1)S(1)} %copy-done, bf16[48,4096]{1,0:T(8,128)(2,1)S(1)} %constant_dynamic-update-slice_fusion.refs_2_, bf16[48,4096]{1,0:T(8,128)(2,1)S(1)} %constant_dynamic-update-slice_fusion.3.refs_3_, ...), custom_call_target="tpu_custom_call" | custom-call | flops 4462739456 | bytes 19922944 | tf_op jit(solution)/shard_map/pallas_call | solution.py:206
  28.8 0.0 collective-permute-done.5.refs_2_
  28.8 3.2 %collective-permute-done.4.refs_1_ = bf16[48,4096]{1,0:T(8,128)(2,1)S(1)} collective-permute-done((bf16[48,4096]{1,0:T(8,128)(2,1)S(1)}, bf16[48,4096]{1,0:T(8,128)(2,1)S(1)}, u32[]{:S(2)}, u32[]{:S(2)}) %collective-permute-start.4) | collective-permute-done | bytes 393248 | tf_op jit(solution)/shard_map/ppermute | solution.py:265
  32.0 0.9 %collective-permute-start.12 = (bf16[48,4096]{1,0:T(8,128)(2,1)S(1)}, bf16[48,4096]{1,0:T(8,128)(2,1)S(1)}, u32[]{:S(2)}, u32[]{:S(2)}) collective-permute-start(bf16[48,4096]{1,0:T(8,128)(2,1)S(1)} %collective-permute-done.4.refs_1_), channel_id=1, source_target_pairs={{0,4},{4,0},{8,12},{12,8},{16,20},{20,16},{24,28},{28,24},{32,36},... | collective-permute-start | bytes 1179656 | tf_op jit(solution)/shard_map/ppermute | solution.py:276
  32.9 0.0 collective-permute-start.13
  32.9 4.3 %shard_map.61.refs_7_ = f32[96,128]{1,0:T(8,128)S(1)} custom-call(s32[1,128]{1,0:T(1,128)S(1)} %shard_map.59.refs_0_, bf16[48,4096]{1,0:T(8,128)(2,1)S(1)} %collective-permute-done.4.refs_1_, bf16[48,4096]{1,0:T(8,128)(2,1)S(1)} %collective-permute-done.5.refs_2_, bf16[4096,2432]{1,0:T(8,128)(2,1)S(1)} %bitcast.4, ...), custom_call_target="tpu_custom_call" | custom-call | flops 1912602624 | bytes 19922944 | tf_op jit(solution)/shard_map/pallas_call | solution.py:206
  37.2 0.0 collective-permute-done.3.refs_2_
  37.2 0.6 %collective-permute-start.14 = (bf16[48,4096]{1,0:T(8,128)(2,1)S(1)}, bf16[48,4096]{1,0:T(8,128)(2,1)S(1)}, u32[]{:S(2)}, u32[]{:S(2)}) collective-permute-start(bf16[48,4096]{1,0:T(8,128)(2,1)S(1)} %collective-permute-done.3.refs_2_), channel_id=1, source_target_pairs={{0,4},{4,0},{8,12},{12,8},{16,20},{20,16},{24,28},{28,24},{32,36},... | collective-permute-start | bytes 1179656 | tf_op jit(solution)/shard_map/ppermute | solution.py:276
  37.8 0.0 collective-permute-done.12.refs_3_
  37.8 0.0 collective-permute-done.13.refs_4_
  37.8 1.3 %collective-permute-done.14.refs_5_ = bf16[48,4096]{1,0:T(8,128)(2,1)S(1)} collective-permute-done((bf16[48,4096]{1,0:T(8,128)(2,1)S(1)}, bf16[48,4096]{1,0:T(8,128)(2,1)S(1)}, u32[]{:S(2)}, u32[]{:S(2)}) %collective-permute-start.14) | collective-permute-done | bytes 393248 | tf_op jit(solution)/shard_map/ppermute | solution.py:276
  39.1 6.2 %shard_map.62 = f32[512,128]{1,0:T(8,128)S(1)} custom-call(s32[1,128]{1,0:T(1,128)S(1)} %shard_map.59.refs_0_, s32[512]{0:T(512)S(1)} %copy-done.2, bf16[48,4096]{1,0:T(8,128)(2,1)S(1)} %collective-permute-done.3.refs_2_, bf16[48,4096]{1,0:T(8,128)(2,1)S(1)} %collective-permute-done.12.refs_3_, bf16[48,4096]{1,0:T(8,128)(2,1)S(1)} %collective-permute-done.13.refs_4_, ...), custom_call_target="tpu_custom_call" | custom-call | flops 3825205248 | bytes 19922944 | tf_op jit(solution)/shard_map/pallas_call | solution.py:206
  45.3 12.1 %all_to_all.5.rows_ref = f32[32,16,128]{2,1,0:T(8,128)S(1)} all-to-all(f32[32,16,128]{2,1,0:T(8,128)S(1)} %bitcast.5), channel_id=1, replica_groups=mesh['vocab'=32,'group'=4] {'vocab'}, dimensions={0} | all-to-all | bytes 524288 | tf_op jit(solution)/shard_map/all_to_all | solution.py:299
  57.4 0.9 %shard_map.63 = (f32[16,64]{1,0:T(8,128)}, f32[1,16]{1,0:T(1,128)}) custom-call(f32[32,16,128]{2,1,0:T(8,128)S(1)} %all_to_all.5.rows_ref), custom_call_target="tpu_custom_call" | custom-call | tf_op jit(solution)/shard_map/pallas_call | solution.py:249
  (11 shorter events, 0.1 us)
Async XLA Ops:
  0.6 9.7 %collective-permute-start.6 = (bf16[16,4096]{1,0:T(8,128)(2,1)}, bf16[16,4096]{1,0:T(8,128)(2,1)S(1)}, u32[]{:S(2)}, u32[]{:S(2)}) collective-permute-start(bf16[16,4096]{1,0:T(8,128)(2,1)} %refs_1_.2), channel_id=1, source_target_pairs={{0,8},{4,36},{8,16},{12,44},{16,24},{20,52},{24,0},{28,60},{32,40}... | collective-permute-start | bytes 393224 | tf_op jit(solution)/shard_map/ppermute | solution.py:265
  2.7 11.1 %collective-permute-start.8 = (bf16[16,4096]{1,0:T(8,128)(2,1)}, bf16[16,4096]{1,0:T(8,128)(2,1)S(1)}, u32[]{:S(2)}, u32[]{:S(2)}) collective-permute-start(bf16[16,4096]{1,0:T(8,128)(2,1)} %refs_1_.2), channel_id=1, source_target_pairs={{0,16},{4,68},{8,24},{12,76},{16,0},{20,84},{24,8},{28,92},{32,48}... | collective-permute-start | bytes 393224 | tf_op jit(solution)/shard_map/ppermute | solution.py:265
  5.2 6.2 %collective-permute-start.7 = (bf16[16,4096]{1,0:T(8,128)(2,1)}, bf16[16,4096]{1,0:T(8,128)(2,1)S(1)}, u32[]{:S(2)}, u32[]{:S(2)}) collective-permute-start(bf16[16,4096]{1,0:T(8,128)(2,1)} %refs_1_.2), channel_id=1, source_target_pairs={{0,24},{4,100},{8,0},{12,108},{16,8},{20,116},{24,16},{28,124},{32... | collective-permute-start | bytes 393224 | tf_op jit(solution)/shard_map/ppermute | solution.py:265
  6.3 9.3 %collective-permute-start.2 = (bf16[16,4096]{1,0:T(8,128)(2,1)}, bf16[16,4096]{1,0:T(8,128)(2,1)S(1)}, u32[]{:S(2)}, u32[]{:S(2)}) collective-permute-start(bf16[16,4096]{1,0:T(8,128)(2,1)} %refs_1_.2), channel_id=1, source_target_pairs={{0,64},{4,20},{8,72},{12,28},{16,80},{20,4},{24,88},{28,12},{32,96... | collective-permute-start | bytes 393224 | tf_op jit(solution)/shard_map/ppermute | solution.py:265
  9.9 5.7 %collective-permute-start.1 = (bf16[16,4096]{1,0:T(8,128)(2,1)}, bf16[16,4096]{1,0:T(8,128)(2,1)S(1)}, u32[]{:S(2)}, u32[]{:S(2)}) collective-permute-start(bf16[16,4096]{1,0:T(8,128)(2,1)} %refs_1_.2), channel_id=1, source_target_pairs={{0,96},{4,28},{8,104},{12,4},{16,112},{20,12},{24,120},{28,20},{32... | collective-permute-start | bytes 393224 | tf_op jit(solution)/shard_map/ppermute | solution.py:265
  10.4 5.2 %collective-permute-start = (bf16[16,4096]{1,0:T(8,128)(2,1)}, bf16[16,4096]{1,0:T(8,128)(2,1)S(1)}, u32[]{:S(2)}, u32[]{:S(2)}) collective-permute-start(bf16[16,4096]{1,0:T(8,128)(2,1)} %refs_1_.2), channel_id=1, source_target_pairs={{0,32},{4,12},{8,40},{12,20},{16,48},{20,28},{24,56},{28,4},{32,64... | collective-permute-start | bytes 393224 | tf_op jit(solution)/shard_map/ppermute | solution.py:265
  11.4 9.6 %collective-permute-start.9 = (bf16[16,4096]{1,0:T(8,128)(2,1)}, bf16[16,4096]{1,0:T(8,128)(2,1)S(1)}, u32[]{:S(2)}, u32[]{:S(2)}) collective-permute-start(bf16[16,4096]{1,0:T(8,128)(2,1)} %refs_1_.2), channel_id=1, source_target_pairs={{0,4},{4,0},{8,12},{12,8},{16,20},{20,16},{24,28},{28,24},{32,36},... | collective-permute-start | bytes 393224 | tf_op jit(solution)/shard_map/ppermute | solution.py:276
  13.9 7.4 %collective-permute-start.11 = (bf16[48,4096]{1,0:T(8,128)(2,1)S(1)}, bf16[48,4096]{1,0:T(8,128)(2,1)S(1)}, u32[]{:S(2)}, u32[]{:S(2)}) collective-permute-start(bf16[48,4096]{1,0:T(8,128)(2,1)S(1)} %constant_dynamic-update-slice_fusion.3.refs_3_), channel_id=1, source_target_pairs={{0,4},{4,0},{8,12},{12,8},{16,20},{20,16},{24,28},{28,24},{32,36},... | collective-permute-start | bytes 1179656 | tf_op jit(solution)/shard_map/ppermute | solution.py:276
  15.7 5.7 %slice-start = ((s8[19922944]{0:T(1024)(128)(4,1)}), s8[4194304]{0:T(1024)(128)(4,1)S(1)}, s32[]{:S(2)}) async-start(s8[19922944]{0:T(1024)(128)(4,1)} %bitcast.3), calls=%async_computation.1 | async-start | bytes 8388608
  15.7 5.7 %slice-start.1 = ((s8[19922944]{0:T(1024)(128)(4,1)}), s8[4194304]{0:T(1024)(128)(4,1)S(1)}, s32[]{:S(2)}) async-start(s8[19922944]{0:T(1024)(128)(4,1)} %bitcast.3), calls=%async_computation.2 | async-start | bytes 8388608
  15.7 5.7 %slice-start.2 = ((s8[19922944]{0:T(1024)(128)(4,1)}), s8[4194304]{0:T(1024)(128)(4,1)S(1)}, s32[]{:S(2)}) async-start(s8[19922944]{0:T(1024)(128)(4,1)} %bitcast.3), calls=%async_computation.3 | async-start | bytes 8388608
  15.7 5.8 %slice-start.3 = ((s8[19922944]{0:T(1024)(128)(4,1)}), s8[4194304]{0:T(1024)(128)(4,1)S(1)}, s32[]{:S(2)}) async-start(s8[19922944]{0:T(1024)(128)(4,1)} %bitcast.3), calls=%async_computation.4 | async-start | bytes 8388608
  15.7 6.7 %slice-start.4 = ((s8[19922944]{0:T(1024)(128)(4,1)}), s8[3145728]{0:T(1024)(128)(4,1)S(1)}, s32[]{:S(2)}) async-start(s8[19922944]{0:T(1024)(128)(4,1)} %bitcast.3), calls=%async_computation.5 | async-start | bytes 6291456
  15.7 6.7 %copy-start = (bf16[16,4096]{1,0:T(8,128)(2,1)S(1)}, bf16[16,4096]{1,0:T(8,128)(2,1)}, u32[]{:S(2)}) copy-start(bf16[16,4096]{1,0:T(8,128)(2,1)} %refs_1_.2) | copy-start | bytes 393220
  15.7 6.7 %copy-start.1 = (s32[512,64]{0,1:T(8,128)S(1)}, s32[512,64]{0,1:T(8,128)}, u32[]{:S(2)}) copy-start(s32[512,64]{0,1:T(8,128)} %param.6) | copy-start | bytes 393220
  15.8 5.6 %collective-permute-start.10 = (bf16[48,4096]{1,0:T(8,128)(2,1)S(1)}, bf16[48,4096]{1,0:T(8,128)(2,1)S(1)}, u32[]{:S(2)}, u32[]{:S(2)}) collective-permute-start(bf16[48,4096]{1,0:T(8,128)(2,1)S(1)} %constant_dynamic-update-slice_fusion.refs_2_), channel_id=1, source_target_pairs={{0,4},{4,0},{8,12},{12,8},{16,20},{20,16},{24,28},{28,24},{32,36},... | collective-permute-start | bytes 1179656 | tf_op jit(solution)/shard_map/ppermute | solution.py:276
  19.5 9.3 %collective-permute-start.5 = (bf16[48,4096]{1,0:T(8,128)(2,1)S(1)}, bf16[48,4096]{1,0:T(8,128)(2,1)S(1)}, u32[]{:S(2)}, u32[]{:S(2)}) collective-permute-start(bf16[48,4096]{1,0:T(8,128)(2,1)S(1)} %constant_dynamic-update-slice_fusion.refs_2_), channel_id=1, source_target_pairs={{0,24},{4,100},{8,0},{12,108},{16,8},{20,116},{24,16},{28,124},{32... | collective-permute-start | bytes 1179656 | tf_op jit(solution)/shard_map/ppermute | solution.py:265
  19.6 12.4 %collective-permute-start.4 = (bf16[48,4096]{1,0:T(8,128)(2,1)S(1)}, bf16[48,4096]{1,0:T(8,128)(2,1)S(1)}, u32[]{:S(2)}, u32[]{:S(2)}) collective-permute-start(bf16[48,4096]{1,0:T(8,128)(2,1)S(1)} %constant_dynamic-update-slice_fusion.refs_2_), channel_id=1, source_target_pairs={{0,8},{4,36},{8,16},{12,44},{16,24},{20,52},{24,0},{28,60},{32,40}... | collective-permute-start | bytes 1179656 | tf_op jit(solution)/shard_map/ppermute | solution.py:265
  21.1 16.1 %collective-permute-start.3 = (bf16[48,4096]{1,0:T(8,128)(2,1)S(1)}, bf16[48,4096]{1,0:T(8,128)(2,1)S(1)}, u32[]{:S(2)}, u32[]{:S(2)}) collective-permute-start(bf16[48,4096]{1,0:T(8,128)(2,1)S(1)} %constant_dynamic-update-slice_fusion.refs_2_), channel_id=1, source_target_pairs={{0,16},{4,68},{8,24},{12,76},{16,0},{20,84},{24,8},{28,92},{32,48}... | collective-permute-start | bytes 1179656 | tf_op jit(solution)/shard_map/ppermute | solution.py:265
  22.4 16.7 %copy-start.2 = (s32[512]{0:T(512)S(1)}, s32[512]{0:T(512)}, u32[]{:S(2)}) copy-start(s32[512]{0:T(512)} %refs_1_.3) | copy-start | bytes 6148
  32.0 5.7 %collective-permute-start.12 = (bf16[48,4096]{1,0:T(8,128)(2,1)S(1)}, bf16[48,4096]{1,0:T(8,128)(2,1)S(1)}, u32[]{:S(2)}, u32[]{:S(2)}) collective-permute-start(bf16[48,4096]{1,0:T(8,128)(2,1)S(1)} %collective-permute-done.4.refs_1_), channel_id=1, source_target_pairs={{0,4},{4,0},{8,12},{12,8},{16,20},{20,16},{24,28},{28,24},{32,36},... | collective-permute-start | bytes 1179656 | tf_op jit(solution)/shard_map/ppermute | solution.py:276
  32.9 4.9 %collective-permute-start.13 = (bf16[48,4096]{1,0:T(8,128)(2,1)S(1)}, bf16[48,4096]{1,0:T(8,128)(2,1)S(1)}, u32[]{:S(2)}, u32[]{:S(2)}) collective-permute-start(bf16[48,4096]{1,0:T(8,128)(2,1)S(1)} %collective-permute-done.5.refs_2_), channel_id=1, source_target_pairs={{0,4},{4,0},{8,12},{12,8},{16,20},{20,16},{24,28},{28,24},{32,36},... | collective-permute-start | bytes 1179656 | tf_op jit(solution)/shard_map/ppermute | solution.py:276
  37.2 1.9 %collective-permute-start.14 = (bf16[48,4096]{1,0:T(8,128)(2,1)S(1)}, bf16[48,4096]{1,0:T(8,128)(2,1)S(1)}, u32[]{:S(2)}, u32[]{:S(2)}) collective-permute-start(bf16[48,4096]{1,0:T(8,128)(2,1)S(1)} %collective-permute-done.3.refs_2_), channel_id=1, source_target_pairs={{0,4},{4,0},{8,12},{12,8},{16,20},{20,16},{24,28},{28,24},{32,36},... | collective-permute-start | bytes 1179656 | tf_op jit(solution)/shard_map/ppermute | solution.py:276

commit v3 on v1

--- a/solution.py
+++ b/solution.py
@@ -99,8 +99,10 @@
             some = picks_ref[:, left : left + LANES]
             more = jnp.full((LANES - picks, LANES), -1, jnp.int32)
             index_ref[left : left + LANES, :] = jnp.concatenate([some, more], axis=0).T
+    if len(x_refs) == 1:
+        x_all = x_refs[0]
     at = 0
-    for x_ref in x_refs:
+    for x_ref in x_refs if len(x_refs) > 1 else ():
         x_all[at : at + x_ref.shape[0], :] = x_ref[...]
         at += x_ref.shape[0]
     block_rows = index_ref.shape[0] // (RING * RING * CORES)
@@ -278,13 +280,14 @@
     at = list(range(shard_count))
     cut = 2 * EARLY, 2 * EARLY + LATE
     others = [swapped(v) for v in early.values()]
-    xs = [*early.values(), *others]
+    xs = [jnp.concatenate([*early.values(), *others])]
     first, index = chunk(blocks, xs, at[: cut[0]], [], head_weight, pick_index.T, first=True)
     *rest, first = lax.optimization_barrier((*rest, first))
-    second = chunk(blocks, rest, at[cut[0] : cut[1]], [], head_weight, index)
-    others = [swapped(v) for v in rest]
+    late = jnp.concatenate(rest)
+    second = chunk(blocks, [late], at[cut[0] : cut[1]], [], head_weight, index)
+    others = swapped(late)
     held = [first, second]
-    rows = chunk(blocks, others, at[cut[1] :], held, head_weight, index, order=owner_order)
+    rows = chunk(blocks, [others], at[cut[1] :], held, head_weight, index, order=owner_order)
     rows = rows.reshape(shard_count, own_rows, LANES)
     received = lax.all_to_all(rows, AXIS, split_axis=0, concat_axis=0, tiled=True)
     return combine(received, pick_count)

time: 56.1 us -> 53.6 us (0.955)
  waiting for transfers between devices: 5.08 us -> 1.32 us
  blocking collectives: 12 us -> 13.7 us
  local copies, waits for them, and re-layouts: 1.09 us -> 0.26 us
  starting transfers between devices: 20.3 us -> 20.9 us
    ppermute x9, waiting for transfers between devices: 5.06 us -> 0.02 us  [shifts(): received.append(lax.ppermute(value, AXIS, along(k, phase)))]
    all_to_all x1, blocking collectives: 12 us -> 13.7 us  [program(): lax.all_to_all(rows, AXIS, split_axis=0, concat_axis=0, tiled=True)]
    ppermute x6 -> x4, waiting for transfers between devices: 0.02 us -> 1.3 us  [swapped(): return lax.ppermute(value, AXIS, swap)]
    unnamed x20 -> x19, local copies, waits for them, and re-layouts: 1.07 us -> 0.21 us
    ppermute x9, starting transfers between devices: 12.6 us -> 13.4 us  [shifts(): received.append(lax.ppermute(value, AXIS, along(k, phase)))]
    ppermute x6 -> x4, starting transfers between devices: 7.65 us -> 7.52 us  [swapped(): return lax.ppermute(value, AXIS, swap)]
  transfers between devices with their start and end apart: 15 -> 13, of which waited for: 3 -> 1; matrix products, arithmetic and copies ran while one was open for 0% -> 0% of each run, Pallas kernels for 19% -> 20%
where the time goes in v3:
time: 53.6 us; the launch traced here: 53.4 us
  starting transfers between devices  20.9 us (39%)
  Pallas kernels  16.3 us (30%)
  blocking collectives  13.7 us (26%)
  waiting for transfers between devices  1.32 us (2%)
  between operations  0.86 us (2%)
    pallas_call x3, Pallas kernels, chunk(): pl.pallas_call(functools.partial(chunk_kernel, pieces=len(xs), blocks=mem...  15.4 us
    all_to_all x1, blocking collectives, program(): lax.all_to_all(rows, AXIS, split_axis=0, concat_axis=0, tiled=True)  13.7 us
    ppermute x9, starting transfers between devices, shifts(): received.append(lax.ppermute(value, AXIS, along(k, phase)))  13.4 us
    ppermute x4, starting transfers between devices, swapped(): return lax.ppermute(value, AXIS, swap)  7.52 us
    ppermute x4, waiting for transfers between devices, swapped(): return lax.ppermute(value, AXIS, swap)  1.3 us
  transfers between devices with their start and end apart: 13, of which 1 were waited for; matrix products, arithmetic and copies ran while one was open for 0% of the time, Pallas kernels for 20%

profile of v3, /device:TPU:1, one launch (start us, length us, event | category | flops | bytes accessed | tf_op | source)
XLA Modules:
  0.0 53.4 jit_solution(2675234566005909628)
XLA Ops:
  0.6 0.0 copy-start.3
  0.6 2.5 %collective-permute-start = (bf16[16,4096]{1,0:T(8,128)(2,1)}, bf16[16,4096]{1,0:T(8,128)(2,1)S(1)}, u32[]{:S(2)}, u32[]{:S(2)}) collective-permute-start(bf16[16,4096]{1,0:T(8,128)(2,1)} %param.4), channel_id=1, source_target_pairs={{0,32},{4,12},{8,40},{12,20},{16,48},{20,28},{24,56},{28,4},{32,64... | collective-permute-start | bytes 393224 | tf_op jit(solution)/shard_map/ppermute | solution.py:261
  3.2 2.2 %collective-permute-start.1 = (bf16[16,4096]{1,0:T(8,128)(2,1)}, bf16[16,4096]{1,0:T(8,128)(2,1)S(1)}, u32[]{:S(2)}, u32[]{:S(2)}) collective-permute-start(bf16[16,4096]{1,0:T(8,128)(2,1)} %param.4), channel_id=1, source_target_pairs={{0,96},{4,28},{8,104},{12,4},{16,112},{20,12},{24,120},{28,20},{32... | collective-permute-start | bytes 393224 | tf_op jit(solution)/shard_map/ppermute | solution.py:261
  5.4 1.2 %collective-permute-start.2 = (bf16[16,4096]{1,0:T(8,128)(2,1)}, bf16[16,4096]{1,0:T(8,128)(2,1)S(1)}, u32[]{:S(2)}, u32[]{:S(2)}) collective-permute-start(bf16[16,4096]{1,0:T(8,128)(2,1)} %param.4), channel_id=1, source_target_pairs={{0,64},{4,20},{8,72},{12,28},{16,80},{20,4},{24,88},{28,12},{32,96... | collective-permute-start | bytes 393224 | tf_op jit(solution)/shard_map/ppermute | solution.py:261
  6.6 1.2 %collective-permute-start.6 = (bf16[16,4096]{1,0:T(8,128)(2,1)}, bf16[16,4096]{1,0:T(8,128)(2,1)S(1)}, u32[]{:S(2)}, u32[]{:S(2)}) collective-permute-start(bf16[16,4096]{1,0:T(8,128)(2,1)} %param.4), channel_id=1, source_target_pairs={{0,8},{4,36},{8,16},{12,44},{16,24},{20,52},{24,0},{28,60},{32,40}... | collective-permute-start | bytes 393224 | tf_op jit(solution)/shard_map/ppermute | solution.py:261
  7.8 1.5 %collective-permute-start.7 = (bf16[16,4096]{1,0:T(8,128)(2,1)}, bf16[16,4096]{1,0:T(8,128)(2,1)S(1)}, u32[]{:S(2)}, u32[]{:S(2)}) collective-permute-start(bf16[16,4096]{1,0:T(8,128)(2,1)} %param.4), channel_id=1, source_target_pairs={{0,24},{4,100},{8,0},{12,108},{16,8},{20,116},{24,16},{28,124},{32... | collective-permute-start | bytes 393224 | tf_op jit(solution)/shard_map/ppermute | solution.py:261
  9.3 0.0 copy-start
  9.3 0.0 copy-done.3
  9.3 0.0 collective-permute-done
  9.3 1.6 %collective-permute-start.8 = (bf16[16,4096]{1,0:T(8,128)(2,1)S(1)}, bf16[16,4096]{1,0:T(8,128)(2,1)S(1)}, u32[]{:S(2)}, u32[]{:S(2)}) collective-permute-start(bf16[16,4096]{1,0:T(8,128)(2,1)S(1)} %copy-done.3), channel_id=1, source_target_pairs={{0,16},{4,68},{8,24},{12,76},{16,0},{20,84},{24,8},{28,92},{32,48}... | collective-permute-start | bytes 393224 | tf_op jit(solution)/shard_map/ppermute | solution.py:261
  11.0 0.0 collective-permute-done.1
  11.0 2.4 %collective-permute-start.9 = (bf16[16,4096]{1,0:T(8,128)(2,1)S(1)}, bf16[16,4096]{1,0:T(8,128)(2,1)S(1)}, u32[]{:S(2)}, u32[]{:S(2)}) collective-permute-start(bf16[16,4096]{1,0:T(8,128)(2,1)S(1)} %copy-done.3), channel_id=1, source_target_pairs={{0,4},{4,0},{8,12},{12,8},{16,20},{20,16},{24,28},{28,24},{32,36},... | collective-permute-start | bytes 393224 | tf_op jit(solution)/shard_map/ppermute | solution.py:272
  13.4 0.0 collective-permute-done.2
  13.4 0.0 copy-start.1
  13.5 0.1 collective-permute-start.10
  13.6 0.0 collective-permute-done.6
  13.6 0.4 collective-permute-start.3
  14.0 0.0 collective-permute-done.7
  14.0 2.4 %collective-permute-start.4 = (bf16[48,4096]{1,0:T(8,128)(2,1)S(1)}, bf16[48,4096]{1,0:T(8,128)(2,1)S(1)}, u32[]{:S(2)}, u32[]{:S(2)}) collective-permute-start(bf16[48,4096]{1,0:T(8,128)(2,1)S(1)} %get-tuple-element.19), channel_id=1, source_target_pairs={{0,24},{4,100},{8,0},{12,108},{16,8},{20,116},{24,16},{28,124},{32... | collective-permute-start | bytes 1179656 | tf_op jit(solution)/shard_map/ppermute | solution.py:261
  16.4 0.0 collective-permute-done.8
  16.4 0.3 collective-permute-start.5
  16.8 0.0 collective-permute-done.9
  16.8 3.1 %collective-permute-start.11 = (bf16[48,4096]{1,0:T(8,128)(2,1)S(1)}, bf16[48,4096]{1,0:T(8,128)(2,1)S(1)}, u32[]{:S(2)}, u32[]{:S(2)}) collective-permute-start(bf16[48,4096]{1,0:T(8,128)(2,1)S(1)} %pad_maximum_fusion), channel_id=1, source_target_pairs={{0,4},{4,0},{8,12},{12,8},{16,20},{20,16},{24,28},{28,24},{32,36},... | collective-permute-start | bytes 1179656 | tf_op jit(solution)/shard_map/ppermute | solution.py:272
  20.0 0.0 collective-permute-done.10
  20.0 1.3 %collective-permute-done.11 = bf16[48,4096]{1,0:T(8,128)(2,1)S(1)} collective-permute-done((bf16[48,4096]{1,0:T(8,128)(2,1)S(1)}, bf16[48,4096]{1,0:T(8,128)(2,1)S(1)}, u32[]{:S(2)}, u32[]{:S(2)}) %collective-permute-start.11) | collective-permute-done | bytes 393248 | tf_op jit(solution)/shard_map/ppermute | solution.py:272
  21.3 0.0 copy-done
  21.3 0.0 copy-done.1
  21.4 6.2 %shard_map.60 = (f32[224,128]{1,0:T(8,128)S(1)}, s32[512,128]{1,0:T(8,128)S(1)}) custom-call(s32[1,128]{1,0:T(1,128)S(1)} %shard_map.59.refs_0_, bf16[224,4096]{1,0:T(8,128)(2,1)S(1)} %constant_dynamic-update-slice_fusion.3.refs_1_, bf16[4096,2432]{1,0:T(8,128)(2,1)S(1)} %copy-done, s32[64,512]{1,0:T(8,128)S(1)} %bitcast.4), custom_call_target="tpu_custom_call" | custom-call | flops 4462739456 | bytes 19922944 | tf_op jit(solution)/shard_map/pallas_call | solution.py:202
  27.6 0.0 collective-permute-done.3
  27.6 0.0 collective-permute-done.4
  27.6 0.0 collective-permute-done.5
  27.7 1.8 %collective-permute-start.12 = (bf16[144,4096]{1,0:T(8,128)(2,1)S(1)}, bf16[144,4096]{1,0:T(8,128)(2,1)S(1)}, u32[]{:S(2)}, u32[]{:S(2)}) collective-permute-start(bf16[144,4096]{1,0:T(8,128)(2,1)S(1)} %constant_dynamic-update-slice_fusion.13.refs_1_), channel_id=1, source_target_pairs={{0,4},{4,0},{8,12},{12,8},{16,20},{20,16},{24,28},{28,24},{32,36},... | collective-permute-start | bytes 3538952 | tf_op jit(solution)/shard_map/ppermute | solution.py:272
  29.5 0.0 copy-start.2
  29.6 4.3 %shard_map.61.refs_4_ = f32[144,128]{1,0:T(8,128)S(1)} custom-call(s32[1,128]{1,0:T(1,128)S(1)} %shard_map.59.refs_0_, bf16[144,4096]{1,0:T(8,128)(2,1)S(1)} %constant_dynamic-update-slice_fusion.13.refs_1_, bf16[4096,2432]{1,0:T(8,128)(2,1)S(1)} %copy-done, s32[512,128]{1,0:T(8,128)S(1)} %get-tuple-element.15.refs_3_.refs_6_), custom_call_target="tpu_custom_call" | custom-call | flops 2868903936 | bytes 19922944 | tf_op jit(solution)/shard_map/pallas_call | solution.py:202
  33.9 0.0 collective-permute-done.12.refs_2_
  33.9 0.0 copy-done.2
  33.9 4.9 %shard_map.62 = f32[512,128]{1,0:T(8,128)S(1)} custom-call(s32[1,128]{1,0:T(1,128)S(1)} %shard_map.59.refs_0_, s32[512]{0:T(512)S(1)} %copy-done.2, bf16[144,4096]{1,0:T(8,128)(2,1)S(1)} %collective-permute-done.12.refs_2_, f32[224,128]{1,0:T(8,128)S(1)} %get-tuple-element.14.refs_3_, f32[144,128]{1,0:T(8,128)S(1)} %shard_map.61.refs_4_, ...), custom_call_target="tpu_custom_call" | custom-call | flops 2868903936 | bytes 19922944 | tf_op jit(solution)/shard_map/pallas_call | solution.py:202
  38.8 13.7 %all_to_all.5.rows_ref = f32[32,16,128]{2,1,0:T(8,128)S(1)} all-to-all(f32[32,16,128]{2,1,0:T(8,128)S(1)} %bitcast.3), channel_id=1, replica_groups=mesh['vocab'=32,'group'=4] {'vocab'}, dimensions={0} | all-to-all | bytes 524288 | tf_op jit(solution)/shard_map/all_to_all | solution.py:292
  52.5 0.9 %shard_map.63 = (f32[16,64]{1,0:T(8,128)}, f32[1,16]{1,0:T(1,128)}) custom-call(f32[32,16,128]{2,1,0:T(8,128)S(1)} %all_to_all.5.rows_ref), custom_call_target="tpu_custom_call" | custom-call | tf_op jit(solution)/shard_map/pallas_call | solution.py:245
  (15 shorter events, 0.3 us)
Async XLA Ops:
  0.6 8.7 %copy-start.3 = (bf16[16,4096]{1,0:T(8,128)(2,1)S(1)}, bf16[16,4096]{1,0:T(8,128)(2,1)}, u32[]{:S(2)}) copy-start(bf16[16,4096]{1,0:T(8,128)(2,1)} %param.4) | copy-start | bytes 393220
  0.6 8.7 %collective-permute-start = (bf16[16,4096]{1,0:T(8,128)(2,1)}, bf16[16,4096]{1,0:T(8,128)(2,1)S(1)}, u32[]{:S(2)}, u32[]{:S(2)}) collective-permute-start(bf16[16,4096]{1,0:T(8,128)(2,1)} %param.4), channel_id=1, source_target_pairs={{0,32},{4,12},{8,40},{12,20},{16,48},{20,28},{24,56},{28,4},{32,64... | collective-permute-start | bytes 393224 | tf_op jit(solution)/shard_map/ppermute | solution.py:261
  3.2 7.8 %collective-permute-start.1 = (bf16[16,4096]{1,0:T(8,128)(2,1)}, bf16[16,4096]{1,0:T(8,128)(2,1)S(1)}, u32[]{:S(2)}, u32[]{:S(2)}) collective-permute-start(bf16[16,4096]{1,0:T(8,128)(2,1)} %param.4), channel_id=1, source_target_pairs={{0,96},{4,28},{8,104},{12,4},{16,112},{20,12},{24,120},{28,20},{32... | collective-permute-start | bytes 393224 | tf_op jit(solution)/shard_map/ppermute | solution.py:261
  5.4 8.1 %collective-permute-start.2 = (bf16[16,4096]{1,0:T(8,128)(2,1)}, bf16[16,4096]{1,0:T(8,128)(2,1)S(1)}, u32[]{:S(2)}, u32[]{:S(2)}) collective-permute-start(bf16[16,4096]{1,0:T(8,128)(2,1)} %param.4), channel_id=1, source_target_pairs={{0,64},{4,20},{8,72},{12,28},{16,80},{20,4},{24,88},{28,12},{32,96... | collective-permute-start | bytes 393224 | tf_op jit(solution)/shard_map/ppermute | solution.py:261
  6.6 7.0 %collective-permute-start.6 = (bf16[16,4096]{1,0:T(8,128)(2,1)}, bf16[16,4096]{1,0:T(8,128)(2,1)S(1)}, u32[]{:S(2)}, u32[]{:S(2)}) collective-permute-start(bf16[16,4096]{1,0:T(8,128)(2,1)} %param.4), channel_id=1, source_target_pairs={{0,8},{4,36},{8,16},{12,44},{16,24},{20,52},{24,0},{28,60},{32,40}... | collective-permute-start | bytes 393224 | tf_op jit(solution)/shard_map/ppermute | solution.py:261
  7.8 6.2 %collective-permute-start.7 = (bf16[16,4096]{1,0:T(8,128)(2,1)}, bf16[16,4096]{1,0:T(8,128)(2,1)S(1)}, u32[]{:S(2)}, u32[]{:S(2)}) collective-permute-start(bf16[16,4096]{1,0:T(8,128)(2,1)} %param.4), channel_id=1, source_target_pairs={{0,24},{4,100},{8,0},{12,108},{16,8},{20,116},{24,16},{28,124},{32... | collective-permute-start | bytes 393224 | tf_op jit(solution)/shard_map/ppermute | solution.py:261
  9.3 12.1 %copy-start = (bf16[4096,2432]{1,0:T(8,128)(2,1)S(1)}, bf16[4096,2432]{1,0:T(8,128)(2,1)}, u32[]{:S(2)}) copy-start(bf16[4096,2432]{1,0:T(8,128)(2,1)} %refs_5_.1) | copy-start | bytes 59768836
  9.3 7.1 %collective-permute-start.8 = (bf16[16,4096]{1,0:T(8,128)(2,1)S(1)}, bf16[16,4096]{1,0:T(8,128)(2,1)S(1)}, u32[]{:S(2)}, u32[]{:S(2)}) collective-permute-start(bf16[16,4096]{1,0:T(8,128)(2,1)S(1)} %copy-done.3), channel_id=1, source_target_pairs={{0,16},{4,68},{8,24},{12,76},{16,0},{20,84},{24,8},{28,92},{32,48}... | collective-permute-start | bytes 393224 | tf_op jit(solution)/shard_map/ppermute | solution.py:261
  11.0 5.8 %collective-permute-start.9 = (bf16[16,4096]{1,0:T(8,128)(2,1)S(1)}, bf16[16,4096]{1,0:T(8,128)(2,1)S(1)}, u32[]{:S(2)}, u32[]{:S(2)}) collective-permute-start(bf16[16,4096]{1,0:T(8,128)(2,1)S(1)} %copy-done.3), channel_id=1, source_target_pairs={{0,4},{4,0},{8,12},{12,8},{16,20},{20,16},{24,28},{28,24},{32,36},... | collective-permute-start | bytes 393224 | tf_op jit(solution)/shard_map/ppermute | solution.py:272
  13.4 7.9 %copy-start.1 = (s32[512,64]{0,1:T(8,128)S(1)}, s32[512,64]{0,1:T(8,128)}, u32[]{:S(2)}) copy-start(s32[512,64]{0,1:T(8,128)} %param.6) | copy-start | bytes 393220
  13.5 6.5 %collective-permute-start.10 = (bf16[48,4096]{1,0:T(8,128)(2,1)S(1)}, bf16[48,4096]{1,0:T(8,128)(2,1)S(1)}, u32[]{:S(2)}, u32[]{:S(2)}) collective-permute-start(bf16[48,4096]{1,0:T(8,128)(2,1)S(1)} %get-tuple-element.19), channel_id=1, source_target_pairs={{0,4},{4,0},{8,12},{12,8},{16,20},{20,16},{24,28},{28,24},{32,36},... | collective-permute-start | bytes 1179656 | tf_op jit(solution)/shard_map/ppermute | solution.py:272
  13.6 14.0 %collective-permute-start.3 = (bf16[48,4096]{1,0:T(8,128)(2,1)S(1)}, bf16[48,4096]{1,0:T(8,128)(2,1)S(1)}, u32[]{:S(2)}, u32[]{:S(2)}) collective-permute-start(bf16[48,4096]{1,0:T(8,128)(2,1)S(1)} %get-tuple-element.19), channel_id=1, source_target_pairs={{0,8},{4,36},{8,16},{12,44},{16,24},{20,52},{24,0},{28,60},{32,40}... | collective-permute-start | bytes 1179656 | tf_op jit(solution)/shard_map/ppermute | solution.py:261
  14.0 13.6 %collective-permute-start.4 = (bf16[48,4096]{1,0:T(8,128)(2,1)S(1)}, bf16[48,4096]{1,0:T(8,128)(2,1)S(1)}, u32[]{:S(2)}, u32[]{:S(2)}) collective-permute-start(bf16[48,4096]{1,0:T(8,128)(2,1)S(1)} %get-tuple-element.19), channel_id=1, source_target_pairs={{0,24},{4,100},{8,0},{12,108},{16,8},{20,116},{24,16},{28,124},{32... | collective-permute-start | bytes 1179656 | tf_op jit(solution)/shard_map/ppermute | solution.py:261
  16.4 11.1 %collective-permute-start.5 = (bf16[48,4096]{1,0:T(8,128)(2,1)S(1)}, bf16[48,4096]{1,0:T(8,128)(2,1)S(1)}, u32[]{:S(2)}, u32[]{:S(2)}) collective-permute-start(bf16[48,4096]{1,0:T(8,128)(2,1)S(1)} %get-tuple-element.19), channel_id=1, source_target_pairs={{0,16},{4,68},{8,24},{12,76},{16,0},{20,84},{24,8},{28,92},{32,48}... | collective-permute-start | bytes 1179656 | tf_op jit(solution)/shard_map/ppermute | solution.py:261
  16.8 4.5 %collective-permute-start.11 = (bf16[48,4096]{1,0:T(8,128)(2,1)S(1)}, bf16[48,4096]{1,0:T(8,128)(2,1)S(1)}, u32[]{:S(2)}, u32[]{:S(2)}) collective-permute-start(bf16[48,4096]{1,0:T(8,128)(2,1)S(1)} %pad_maximum_fusion), channel_id=1, source_target_pairs={{0,4},{4,0},{8,12},{12,8},{16,20},{20,16},{24,28},{28,24},{32,36},... | collective-permute-start | bytes 1179656 | tf_op jit(solution)/shard_map/ppermute | solution.py:272
  27.7 6.2 %collective-permute-start.12 = (bf16[144,4096]{1,0:T(8,128)(2,1)S(1)}, bf16[144,4096]{1,0:T(8,128)(2,1)S(1)}, u32[]{:S(2)}, u32[]{:S(2)}) collective-permute-start(bf16[144,4096]{1,0:T(8,128)(2,1)S(1)} %constant_dynamic-update-slice_fusion.13.refs_1_), channel_id=1, source_target_pairs={{0,4},{4,0},{8,12},{12,8},{16,20},{20,16},{24,28},{28,24},{32,36},... | collective-permute-start | bytes 3538952 | tf_op jit(solution)/shard_map/ppermute | solution.py:272
  29.5 4.4 %copy-start.2 = (s32[512]{0:T(512)S(1)}, s32[512]{0:T(512)}, u32[]{:S(2)}) copy-start(s32[512]{0:T(512)} %refs_1_.1) | copy-start | bytes 6148
